TPU v7x, 32 devices: a whole 2x2x4 slice. The times are simulated.
32 devices in a mesh: group: 2 (over x), patch: 16 (over z, y, core).
Axes of the slice: x: 2, y: 2, z: 4, core: 2. Of those that a mesh axis runs over, the one named last changes fastest.
Arguments:
- features: bfloat16 [32, 64, 4, 2304], P(('group', 'patch')), parts along dimension 0, may hold values from -6 to 6
- w_in: bfloat16 [28, 64], replicated, may hold values from -0.75 to 0.75
- w_plane: bfloat16 [9, 28, 28], replicated, may hold values from -0.375 to 0.375
- w_depth: bfloat16 [3, 28, 28], replicated, may hold values from -0.625 to 0.625
- w_head: bfloat16 [3, 28], replicated, may hold values from -1 to 1
- brick_owner: int32 [32], P(('group', 'patch')), parts along dimension 0, may hold values from 0 to 15, each once
- patch_anchor: int32 [32], P(('group', 'patch')), parts along dimension 0, may hold values from 0 to 3, as said below
- aug_code: int32 [32], P(('group', 'patch')), parts along dimension 0, may hold values from 0 to 7, as said below
Outputs:
- blended: float32 [32, 4, 2304], P(('group', 'patch')), parts along dimension 0
There are 2 independent parts, one for each index of `group`. A program takes and returns all parts, laid end to end along the dimension named above; an argument that names none is the same for every part. Nothing has to cross between parts.
Inputs may be any that keep to these rules, and one draw needn't show every extreme that they name: `brick_owner`: every device owns exactly one brick of its region. `patch_anchor`: devices 8 k to 8 k + 7 share one anchor; different positions have different anchors. `aug_code`: devices 8 k to 8 k + 7 hold each code once.
All inputs are finite; a program needn't handle non-finite values.
Results may differ from a plain program's by a relative error of at most 0.00048.
Values sent between devices are 32-bit elements; how exact they have to be, the bound alone decides.
No kernel may reach another device: no remote copies, remote signals or barrier semaphores. Data moves between devices by JAX's collectives and lax.ppermute only.
A program may use at most 64 MiB of HBM per device.

v0:
```python
import functools
import math

import numpy as np

import jax
import jax.numpy as jnp
from jax import lax
from jax.experimental import pallas as pl
from jax.experimental.pallas import tpu as pltpu
from jax.sharding import PartitionSpec as P


F32 = jnp.float32
BF16 = jnp.bfloat16
I32 = jnp.int32
PAD = 32
LANES = 128
SPARE = 96


def iota(shape, axis):
    return lax.broadcasted_iota(I32, shape, axis)


def vmem():
    return pl.BlockSpec(memory_space=pltpu.VMEM)


def smem():
    return pl.BlockSpec(memory_space=pltpu.SMEM)


def hbm():
    return pl.BlockSpec(memory_space=pltpu.HBM)


def stay(*arrays):
    return [pltpu.with_memory_space_constraint(a, pltpu.HBM) for a in arrays]


def params():
    return pltpu.CompilerParams(vmem_limit_bytes=16 * 2**20)


def cost(flops):
    return pl.CostEstimate(flops=flops, bytes_accessed=2**20, transcendentals=0)


def bump(length):
    position = (np.arange(length, dtype=np.float64) + 0.5) / length
    return 0.1 + np.sin(np.pi * position) ** 2


def front_kernel(half, aug_ref, w_in_hbm, w_plane_hbm, w_depth_hbm, w_head_hbm, x_hbm, plane_ref, depth_ref, head_ref, xs_ref, w_in_ref, w_plane_ref, w_depth_ref, w_head_ref, x_ref, big_ref, plane_scr, depth_scr, sems):
    pairs = ((w_plane_hbm, w_plane_ref), (w_in_hbm, w_in_ref), (w_depth_hbm, w_depth_ref), (w_head_hbm, w_head_ref), (x_hbm, x_ref))
    copies = [pltpu.make_async_copy(src, dst, sems.at[k]) for k, (src, dst) in enumerate(pairs)]
    for copy in copies:
        copy.start()
    for copy in copies[:-1]:
        copy.wait()
    hidden, _ = w_in_ref.shape
    depth = depth_ref.shape[0] // PAD
    maps = w_head_ref.shape[0]
    aug = aug_ref[0]
    zf, yf, xf = aug & 1, (aug >> 1) & 1, (aug >> 2) & 1

    rows, cols = big_ref.shape
    spread = (iota((rows, hidden), 0) % PAD == iota((rows, hidden), 1)).astype(BF16)
    gather = (iota((w_in_ref.shape[1], cols), 1) // depth == iota((w_in_ref.shape[1], cols), 0)).astype(BF16)
    tall = jnp.dot(spread, w_in_ref[...], preferred_element_type=F32).astype(BF16)
    wide = jnp.dot(tall, gather, preferred_element_type=F32)
    same = iota((rows, cols), 1) % depth == iota((rows, cols), 0) // PAD
    big_ref[...] = jnp.where(same, wide, 0.0).astype(BF16)

    plane_scr[...] = jnp.zeros_like(plane_scr)
    taps = [w_plane_ref[t].astype(F32) for t in range(9)]
    near = (((0,), (1, 2), ()), ((), (0, 1), (2,)))
    for py in range(2):
        for px in range(2):
            for dy in range(2):
                for dx in range(3):
                    hit = [taps[3 * ty + tx] for ty in near[py][dy + py] for tx in near[px][dx]]
                    if not hit:
                        continue
                    total = functools.reduce(lambda a, b: a + b, hit)
                    high = total.astype(BF16).astype(F32)
                    col = (3 * dy + dx) * PAD
                    plane_scr[py, pl.ds(px * PAD, hidden), pl.ds(col, hidden)] = high
                    plane_scr[py, pl.ds((2 + px) * PAD, hidden), pl.ds(col, hidden)] = total - high
    plane_ref[...] = plane_scr[...].astype(BF16)

    depth_scr[...] = jnp.zeros_like(depth_scr)
    for t in range(3):
        tap = w_depth_ref[t].astype(F32)
        for z in range(depth):
            if 0 <= z + t - 1 < depth:
                depth_scr[pl.ds(z * PAD, hidden), pl.ds((z + t - 1) * PAD, hidden)] = tap
    depth_ref[...] = depth_scr[...].astype(BF16)

    rows, cols = head_ref.shape
    pick = (iota((rows, maps), 0) % maps == iota((rows, maps), 1)).astype(BF16)
    tall = jnp.dot(pick, w_head_ref[...], preferred_element_type=F32).astype(BF16)
    gather = (iota((hidden, cols), 1) % PAD == iota((hidden, cols), 0)).astype(BF16)
    wide = jnp.dot(tall, gather, preferred_element_type=F32)
    at = iota((rows, cols), 0) // maps
    came = iota((rows, cols), 1) // PAD
    flip = (2 * yf + xf) * depth + (depth - 1) * zf
    head_ref[...] = jnp.where(at == (came ^ flip), wide, 0.0).astype(BF16)

    copies[-1].wait()
    channels, depth, cells = x_ref.shape
    rows = depth * PAD
    margin = LANES
    x = x_ref[...].reshape(channels * depth, cells)
    projected = jnp.dot(big_ref[...], x, preferred_element_type=F32).astype(BF16)
    zeros = jnp.zeros((rows, margin), BF16)
    padded = jnp.concatenate([zeros, projected, zeros], axis=1)
    column = iota((rows, cells), 1) % half
    for d in range(3):
        shifted = projected if d == 1 else lax.slice_in_dim(padded, margin + d - 1, margin + d - 1 + cells, axis=1)
        if d == 0:
            shifted = jnp.where(column == 0, jnp.zeros_like(shifted), shifted)
        if d == 2:
            shifted = jnp.where(column == half - 1, jnp.zeros_like(shifted), shifted)
        xs_ref[d, :, pl.ds(0, margin)] = zeros
        xs_ref[d, :, pl.ds(margin, cells)] = shifted
        xs_ref[d, :, pl.ds(margin + cells, margin)] = zeros


def front(aug_code, w_in, w_plane, w_depth, w_head, feat):
    _, channels = w_in.shape
    maps = w_head.shape[0]
    _, depth, cells = feat.shape
    plane = (2, 4 * PAD, 6 * PAD)
    depth_w = (depth * PAD, depth * PAD)
    head = (4 * depth * maps, 4 * depth * PAD)
    shifted = (3, depth * PAD, cells + 2 * LANES)
    return pl.pallas_call(
        functools.partial(front_kernel, math.isqrt(cells)),
        out_shape=[jax.ShapeDtypeStruct(s, BF16) for s in (plane, depth_w, head, shifted)],
        in_specs=[smem()] + [hbm()] * 5,
        out_specs=[vmem()] * 4,
        scratch_shapes=[
            pltpu.VMEM(w_in.shape, BF16),
            pltpu.VMEM(w_plane.shape, BF16),
            pltpu.VMEM(w_depth.shape, BF16),
            pltpu.VMEM(w_head.shape, BF16),
            pltpu.VMEM(feat.shape, BF16),
            pltpu.VMEM((depth * PAD, channels * depth), BF16),
            pltpu.VMEM(plane, F32),
            pltpu.VMEM(depth_w, F32),
            pltpu.SemaphoreType.DMA((5,)),
        ],
        compiler_params=params(),
        cost_estimate=cost(10**8),
        name="front",
    )(aug_code, *stay(w_in, w_plane, w_depth, w_head, feat))


def patch_kernel(half, tiles, brick_rows, last, aug_ref, xs_ref, plane_ref, depth_ref, head_ref, *refs):
    if last:
        carry_in, _, out_ref, a_ref = refs
    else:
        out_ref, carry_out, a_ref = refs
    _, rows, _ = xs_ref.shape
    depth = rows // PAD
    step = 2 * LANES
    margin = LANES
    first_tile = tiles[0] * (step // LANES) - (1 if last else 0)
    if last:
        a_ref[0] = carry_in[...]

    for t in tiles:
        near = []
        for d in range(3):
            block = xs_ref[d, :, pl.ds(t * step, step + 2 * margin)]
            near.append([lax.slice_in_dim(block, margin + half * e, margin + half * e + step, axis=1) for e in (-1, 0, 1)])
        centre = near[1][1].astype(F32)
        first = [[None] * depth for _ in range(4)]
        for z in range(depth):
            cut = slice(z * PAD, (z + 1) * PAD)
            for py in range(2):
                around = jnp.concatenate([near[d][py + e][cut] for e in range(2) for d in range(3)], axis=0)
                mix = jnp.dot(plane_ref[py], around, preferred_element_type=F32)
                for px in range(2):
                    total = mix[px * PAD : (px + 1) * PAD] + mix[(2 + px) * PAD : (3 + px) * PAD]
                    first[2 * py + px][z] = (centre[cut] + jnp.maximum(total, 0.0)).astype(BF16)
        second = []
        for p in range(4):
            one = jnp.concatenate(first[p], axis=0)
            mix = jnp.dot(depth_ref[...], one, preferred_element_type=F32)
            second.append((one.astype(F32) + jnp.maximum(mix, 0.0)).astype(BF16))
        logits = jnp.zeros((head_ref.shape[0], step), F32)
        for q in range(2):
            pair = jnp.concatenate(second[2 * q : 2 * q + 2], axis=0)
            logits = logits + jnp.dot(head_ref[:, 2 * q * rows : 2 * (q + 1) * rows], pair, preferred_element_type=F32)
        affinity = jax.nn.sigmoid(logits)
        for u in range(step // LANES):
            a_ref[t * (step // LANES) + u - first_tile] = affinity[:, u * LANES : (u + 1) * LANES]

    if not last:
        carry_out[...] = a_ref[(tiles[-1] + 1) * (step // LANES) - 1 - first_tile]

    aug = aug_ref[0]
    yf, xf = (aug >> 1) & 1, (aug >> 2) & 1

    side = half // 4
    tail = side * side - LANES
    row_tiles = head_ref.shape[0] // 8
    lane = iota((8, LANES), 1)

    def source(cell, j, odd):
        yl = cell // side
        xl = cell - yl * side
        y = jnp.where(yf == 1, side - 1 - yl, yl)
        xx = side * j + xl
        xx = jnp.where(xf == 1, half - 1 - xx, xx)
        return y * half + xx + odd * (LANES // 2)

    span = -(-side * half // LANES)
    rest_base = jnp.where(yf == 1, 0, span - 2)
    group = lane // tail
    for odd in range(2):
        for j in range(4):
            src = source(lane, j, odd)
            tile_of, lane_of = src // LANES, src % LANES
            hits = [tile_of == k for k in range(span)]
            rest = source(LANES + lane % tail, j, odd)
            rest_hit = rest // LANES == rest_base
            rest_lane = rest % LANES
            for i in [k for k in brick_rows if k % 2 == odd]:
                base = side * half * i // LANES - first_tile
                brick = (i ^ (3 * yf)) * 4 + j
                packed = jnp.zeros((8, LANES), F32)
                for r in range(row_tiles):
                    cut = pl.ds(8 * r, 8)
                    value = jnp.take_along_axis(a_ref[base, cut], lane_of, axis=1)
                    for k in range(1, span):
                        value = jnp.where(hits[k], jnp.take_along_axis(a_ref[base + k, cut], lane_of, axis=1), value)
                    out_ref[brick, cut] = value
                    low = jnp.take_along_axis(a_ref[base + rest_base, cut], rest_lane, axis=1)
                    high = jnp.take_along_axis(a_ref[base + rest_base + 1, cut], rest_lane, axis=1)
                    packed = jnp.where(group == r, jnp.where(rest_hit, low, high), packed)
                out_ref[brick, pl.ds(8 * row_tiles, 8)] = packed


def patch_half(half, tiles, brick_rows, last, aug_code, shifted, plane, depth_w, head, extra=()):
    kept = head.shape[0]
    bricks = jax.ShapeDtypeStruct((16, kept + 8, LANES), F32)
    carry = jax.ShapeDtypeStruct((kept, LANES), F32)
    return pl.pallas_call(
        functools.partial(patch_kernel, half, tiles, brick_rows, last),
        out_shape=[bricks] if last else [bricks, carry],
        in_specs=[smem()] + [vmem()] * (4 + len(extra)),
        out_specs=[vmem()] if last else [vmem()] * 2,
        scratch_shapes=[pltpu.VMEM((2 * len(tiles) + 1, kept, LANES), F32)],
        input_output_aliases={6: 0} if last else {},
        compiler_params=params(),
        cost_estimate=cost(10**9),
    )(aug_code, shifted, plane, depth_w, head, *extra)


def seed_kernel(owner_ref, out_ref):
    here = iota(out_ref.shape, 1) == lax.axis_index("patch")
    out_ref[...] = jnp.where(here, owner_ref[0], 0)


def seed_table(owner, devices):
    width = -(-devices // LANES) * LANES
    return pl.pallas_call(
        seed_kernel,
        out_shape=jax.ShapeDtypeStruct((1, width), I32),
        in_specs=[smem()],
        out_specs=vmem(),
        compiler_params=params(),
        name="seed",
    )(owner)


def partner(devices, bit):
    return [(d, d ^ bit) for d in range(devices)]


def slots_kernel(devices, bits, table_ref, anchor_ref, mine_ref, other_ref, window_ref, send_ref, keep_ref, place_ref):
    me = lax.axis_index("patch")
    brick_rows = devices // 4

    def note(b, _):
        place_ref[table_ref[0, b]] = b
        return 0

    lax.fori_loop(0, devices, note, 0)
    anchor = anchor_ref[0]
    count = 1 << len(bits)
    _, rows, lanes = mine_ref.shape
    spare = iota((rows, lanes), 1) - jnp.where(iota((rows, lanes), 0) == rows - 8, SPARE, lanes)
    for s in range(count):
        mask = functools.reduce(lambda a, b: a ^ b, [bit for k, bit in enumerate(bits) if s >> (len(bits) - 1 - k) & 1], 0)
        brick = place_ref[me ^ mask]
        row = lax.rem(brick // 4 - anchor + brick_rows, brick_rows)
        at = row * 4 + brick % 4
        if brick_rows > 4:
            at = jnp.where(row < 4, at, 0)
        value = (mine_ref[at] + other_ref[at]) * window_ref[at]
        value = jnp.where(spare == row, 2.0, value)
        value = jnp.where(spare == 4, 2.0 * (brick % 4).astype(F32), value)
        if brick_rows > 4:
            value = jnp.where(row < 4, value, 0.0)
        if s < count // 2:
            keep_ref[s] = value
        else:
            send_ref[s - count // 2] = value


def fill_slots(devices, bits, table, anchor, mine, other, window):
    shape = jax.ShapeDtypeStruct((1 << (len(bits) - 1),) + mine.shape[1:], F32)
    return pl.pallas_call(
        functools.partial(slots_kernel, devices, bits),
        out_shape=[shape, shape],
        in_specs=[smem()] * 2 + [vmem()] * 3,
        out_specs=[vmem()] * 2,
        scratch_shapes=[pltpu.SMEM((devices,), I32)],
        compiler_params=params(),
        name="slots",
    )(table, anchor, mine, other, window)


def brick_kernel(side, maps, depth_curve, mine_ref, other_ref, rows_ref, cols_ref, out_ref):
    depth = len(depth_curve)
    wide = 2 * side
    plane = wide * wide
    tail = side * side - LANES
    per = depth * maps
    brick = mine_ref[0] + other_ref[0]
    kept = 4 * per
    main, packed = brick[:kept], brick[kept:]
    rest = jnp.concatenate([packed if k == 0 else pltpu.roll(packed, LANES - tail * k, 1) for k in range(kept // 8)], axis=0)
    fill = jnp.zeros((16 - per, LANES), F32)
    mains = [jnp.concatenate([main[per * p : per * (p + 1)], fill], axis=0) for p in range(4)]
    rests = [jnp.concatenate([rest[per * p : per * (p + 1)], fill], axis=0) for p in range(4)]
    columns = []
    for d in range(-(-plane // LANES)):
        n = iota((8, LANES), 1) + d * LANES
        y = n // wide
        x = n - y * wide
        cell = (y // 2) * side + x // 2
        quarter = 2 * (y % 2) + x % 2
        lane_of = cell % LANES
        top = min((d + 1) * LANES, plane) - 1
        tiles = []
        for r in range(2):
            cut = slice(8 * r, 8 * r + 8)
            value = None
            for p in range(4):
                one = jnp.take_along_axis(mains[p][cut], lane_of, axis=1)
                if (top // wide // 2 + 1) * side > LANES:
                    one = jnp.where(cell >= LANES, jnp.take_along_axis(rests[p][cut], lane_of, axis=1), one)
                value = one if value is None else jnp.where(quarter == p, one, value)
            tiles.append(value)
        columns.append(jnp.concatenate(tiles, axis=0))
    cells = jnp.concatenate(columns, axis=1)[:, :plane]
    for z in range(depth):
        out_ref[0, pl.ds(0, maps), pl.ds(z * plane, plane)] = cells[z * maps : (z + 1) * maps]

    def noted(k):
        lane = jnp.take_along_axis(packed, jnp.full((8, LANES), SPARE + k, I32), axis=1)[0:1]
        return jnp.concatenate([lane] * (rows_ref.shape[1] // LANES), axis=1)

    counts = [noted(i) for i in range(4)]
    added = counts[0] + counts[1] + counts[2] + counts[3]
    column = noted(4)
    down = sum(counts[i] * rows_ref[pl.ds(i, 1), :] for i in range(4))
    across = sum(jnp.where(column == j * added, cols_ref[pl.ds(j, 1), :], 0.0) for j in range(4))
    window = (down * across)[:, :plane]
    for z in range(depth):
        out_ref[0, pl.ds(maps, 1), pl.ds(z * plane, plane)] = window * depth_curve[z]


def finish(side, maps, depth, mine, other):
    plane = 4 * side * side
    width = -(-plane // LANES) * LANES
    curve = bump(8 * side)
    n = np.arange(width)
    y, x = np.minimum(n // (2 * side), 2 * side - 1), n % (2 * side)
    rows = np.stack([curve[2 * side * i + y] for i in range(4)]).astype(np.float32)
    cols = np.stack([curve[2 * side * i + x] for i in range(4)]).astype(np.float32)
    depth_curve = [float(np.float32(v)) for v in bump(depth)]
    return pl.pallas_call(
        functools.partial(brick_kernel, side, maps, depth_curve),
        out_shape=jax.ShapeDtypeStruct((1, maps + 1, depth * plane), F32),
        in_specs=[vmem()] * 4,
        out_specs=vmem(),
        compiler_params=params(),
        name="brick",
    )(mine, other, rows, cols)


def wire_window(side, maps, depth):
    curve_y, curve_z = bump(8 * side), bump(depth)
    cell = np.arange(side * side)
    out = np.zeros((16, 4 * depth * maps, side * side))
    for i in range(4):
        for j in range(4):
            for p in range(4):
                y = curve_y[2 * side * i + 2 * (cell // side) + p // 2]
                x = curve_y[2 * side * j + 2 * (cell % side) + p % 2]
                for z in range(depth):
                    for m in range(maps):
                        out[4 * i + j, (p * depth + z) * maps + m] = curve_z[z] * y * x
    kept = out.shape[1]
    tail = side * side - LANES
    packed = np.zeros((16, 8, LANES))
    for k in range(kept // 8):
        packed[:, :, tail * k : tail * (k + 1)] = out[:, 8 * k : 8 * k + 8, LANES:]
    return np.concatenate([out[:, :, :LANES], packed], axis=1).astype(np.float32)


def on_device(features, w_in, w_plane, w_depth, w_head, brick_owner, patch_anchor, aug_code):
    devices = lax.axis_size("patch")
    _, _, depth, cells = features.shape
    side = math.isqrt(cells) // 4
    maps = w_head.shape[0]
    bits = [1] + [1 << k | 1 for k in range(1, devices.bit_length() - 1)]

    table = seed_table(brick_owner, devices)
    tables = [table]
    for bit in bits[1:] + bits[:1]:
        got = lax.ppermute(tables[-1], "patch", partner(devices, bit))
        tables.append(tables[-1] + got)
    table = tables[-1]
    plane, depth_w, head, shifted = front(aug_code, w_in, w_plane, w_depth, w_head, features[0])
    half = math.isqrt(cells)
    steps = cells // (2 * LANES)
    ready = -(-half * half // 2 // (2 * LANES))
    bricks, carry = patch_half(half, range(ready), (0, 1), False, aug_code, shifted, plane, depth_w, head)
    (bricks,) = patch_half(half, range(ready, steps), (2, 3), True, aug_code, shifted, plane, depth_w, head, (carry, bricks))
    other = lax.ppermute(bricks, "patch", partner(devices, 1))
    send, keep = fill_slots(devices, bits[1:], table, patch_anchor, bricks, other, wire_window(side, maps, depth))
    for bit in bits[1:-1]:
        got = lax.ppermute(send, "patch", partner(devices, bit))
        half = send.shape[0] // 2
        keep, send = keep[:half] + got[:half], keep[half:] + got[half:]
    other = lax.ppermute(send, "patch", partner(devices, bits[-1]))
    return finish(side, maps, depth, keep, other)


def solution(mesh):
    one = P(("group", "patch"))
    in_specs = (P(("group", "patch"), None, None, None), P(), P(), P(), P(), one, one, one)
    return jax.shard_map(
        on_device, mesh=mesh, in_specs=in_specs, out_specs=P(("group", "patch"), None, None), check_vma=False
    )
```

profile of v0, /device:TPU:0, one launch (start us, length us, event | category | flops | bytes accessed | tf_op | source)
XLA Modules:
  0.0 36.9 jit_solution(10658929725335316368)
XLA Ops:
  0.7 2.0 %front.1 = (bf16[2,128,192]{2,1,0:T(8,128)(2,1)S(1)}, bf16[128,128]{1,0:T(8,128)(2,1)S(1)}, bf16[48,512]{1,0:T(8,128)(2,1)S(1)}, bf16[3,128,2560]{2,1,0:T(8,128)(2,1)S(1)}) custom-call(s32[1]{0:T(128)S(6)} %copy.16.aug_ref, bf16[28,64]{1,0:T(8,128)(2,1)} %w_in_hbm.1, bf16[9,28,28]{2,1,0:T(8,128)(2,1)} %w_plane_hbm.1, bf16[3,28,28]{2,1,0:T(8,128)(2,1)} %w_depth_hbm.1, ...), custom_call_target="tpu_custom_call" | custom-call | flops 100000000 | bytes 1048576 | tf_op jit(solution)/shard_map/front/pallas_call | solution.py:139
  2.6 3.0 %shard_map.109 = (f32[16,56,128]{2,1,0:T(8,128)S(1)}, f32[48,128]{1,0:T(8,128)S(1)}) custom-call(s32[1]{0:T(128)S(6)} %copy.16.aug_ref, bf16[3,128,2560]{2,1,0:T(8,128)(2,1)S(1)} %get-tuple-element.13.xs_ref, bf16[2,128,192]{2,1,0:T(8,128)(2,1)S(1)} %get-tuple-element.14.plane_ref, bf16[128,128]{1,0:T(8,128)(2,1)S(1)} %get-tuple-element.15.depth_ref, ...), custom_call_target="tpu_custom_call" | custom-call | flops 1000000000 | bytes 1048576 | tf_op jit(solution)/shard_map/pallas_call | solution.py:252
  5.7 0.0 copy-start
  5.7 0.0 copy-start.1
  5.7 0.0 copy-start.2
  5.7 2.6 %shard_map.110.mine_ref = f32[16,56,128]{2,1,0:T(8,128)S(1)} custom-call(s32[1]{0:T(128)S(6)} %copy.16.aug_ref, bf16[3,128,2560]{2,1,0:T(8,128)(2,1)S(1)} %get-tuple-element.13.xs_ref, bf16[2,128,192]{2,1,0:T(8,128)(2,1)S(1)} %get-tuple-element.14.plane_ref, bf16[128,128]{1,0:T(8,128)(2,1)S(1)} %get-tuple-element.15.depth_ref, ...), custom_call_target="tpu_custom_call", output_to_operand_aliasing={{}: (6, {})} | custom-call | flops 1000000000 | bytes 1048576 | tf_op jit(solution)/shard_map/pallas_call | solution.py:252
  8.4 0.6 %collective-permute-start.4 = (f32[16,56,128]{2,1,0:T(8,128)S(1)}, f32[16,56,128]{2,1,0:T(8,128)S(1)}, u32[]{:S(2)}, u32[]{:S(2)}) collective-permute-start(f32[16,56,128]{2,1,0:T(8,128)S(1)} %shard_map.110.mine_ref), channel_id=1, source_target_pairs={{0,1},{1,0},{2,3},{3,2},{4,5},{5,4},{6,7},{7,6},{8,9},{9,8},{10,11... | collective-permute-start | bytes 1376264 | tf_op jit(solution)/shard_map/ppermute | solution.py:438
  9.6 2.7 %collective-permute-start = (s32[1,128]{1,0:T(1,128)S(1)}, s32[1,128]{1,0:T(1,128)S(1)}, u32[]{:S(2)}, u32[]{:S(2)}) collective-permute-start(s32[1,128]{1,0:T(1,128)S(1)} %seed.1), channel_id=1, source_target_pairs={{0,3},{1,2},{2,1},{3,0},{4,7},{5,6},{6,5},{7,4},{8,11},{9,10},{10,... | collective-permute-start | bytes 1544 | tf_op jit(solution)/shard_map/ppermute | solution.py:429
  12.3 1.3 %collective-permute-done = s32[1,128]{1,0:T(1,128)S(1)} collective-permute-done((s32[1,128]{1,0:T(1,128)S(1)}, s32[1,128]{1,0:T(1,128)S(1)}, u32[]{:S(2)}, u32[]{:S(2)}) %collective-permute-start) | collective-permute-done | bytes 544 | tf_op jit(solution)/shard_map/ppermute | solution.py:429
  13.6 1.7 %collective-permute-start.1 = (s32[1,128]{1,0:T(1,128)S(1)}, s32[1,128]{1,0:T(1,128)S(1)}, u32[]{:S(2)}, u32[]{:S(2)}) collective-permute-start(s32[1,128]{1,0:T(1,128)S(1)} %add.24), channel_id=1, source_target_pairs={{0,5},{1,4},{2,7},{3,6},{4,1},{5,0},{6,3},{7,2},{8,13},{9,12},{10,... | collective-permute-start | bytes 1544 | tf_op jit(solution)/shard_map/ppermute | solution.py:429
  15.3 1.3 %collective-permute-done.1 = s32[1,128]{1,0:T(1,128)S(1)} collective-permute-done((s32[1,128]{1,0:T(1,128)S(1)}, s32[1,128]{1,0:T(1,128)S(1)}, u32[]{:S(2)}, u32[]{:S(2)}) %collective-permute-start.1) | collective-permute-done | bytes 544 | tf_op jit(solution)/shard_map/ppermute | solution.py:429
  16.6 2.7 %collective-permute-start.2 = (s32[1,128]{1,0:T(1,128)S(1)}, s32[1,128]{1,0:T(1,128)S(1)}, u32[]{:S(2)}, u32[]{:S(2)}) collective-permute-start(s32[1,128]{1,0:T(1,128)S(1)} %add.25), channel_id=1, source_target_pairs={{0,9},{1,8},{2,11},{3,10},{4,13},{5,12},{6,15},{7,14},{8,1},{9,0},... | collective-permute-start | bytes 1544 | tf_op jit(solution)/shard_map/ppermute | solution.py:429
  19.3 1.3 %collective-permute-done.2 = s32[1,128]{1,0:T(1,128)S(1)} collective-permute-done((s32[1,128]{1,0:T(1,128)S(1)}, s32[1,128]{1,0:T(1,128)S(1)}, u32[]{:S(2)}, u32[]{:S(2)}) %collective-permute-start.2) | collective-permute-done | bytes 544 | tf_op jit(solution)/shard_map/ppermute | solution.py:429
  20.6 0.0 collective-permute-start.3
  21.3 0.5 %collective-permute-done.3 = s32[1,128]{1,0:T(1,128)S(1)} collective-permute-done((s32[1,128]{1,0:T(1,128)S(1)}, s32[1,128]{1,0:T(1,128)S(1)}, u32[]{:S(2)}, u32[]{:S(2)}) %collective-permute-start.3) | collective-permute-done | bytes 544 | tf_op jit(solution)/shard_map/ppermute | solution.py:429
  21.8 0.0 collective-permute-done.4.other_ref
  21.8 0.0 copy-done
  21.8 0.8 %slots.1 = (f32[4,56,128]{2,1,0:T(8,128)S(1)}, f32[4,56,128]{2,1,0:T(8,128)S(1)}) custom-call(s32[1,128]{1,0:T(1,128)S(1)} %add.27.table_ref, s32[1]{0:T(128)S(6)} %copy.15.anchor_ref, f32[16,56,128]{2,1,0:T(8,128)S(1)} %shard_map.110.mine_ref, f32[16,56,128]{2,1,0:T(8,128)S(1)} %collective-permute-done.4.other_ref, f32[16,56,128]{2,1,0:T(8,128)S(1)} %copy-done), custom_call_target="tpu_custom_call" | custom-call | tf_op jit(solution)/shard_map/slots/pallas_call | solution.py:318
  22.6 1.6 %collective-permute-start.5 = (f32[4,56,128]{2,1,0:T(8,128)S(1)}, f32[4,56,128]{2,1,0:T(8,128)S(1)}, u32[]{:S(2)}, u32[]{:S(2)}) collective-permute-start(f32[4,56,128]{2,1,0:T(8,128)S(1)} %get-tuple-element.20), channel_id=1, source_target_pairs={{0,3},{1,2},{2,1},{3,0},{4,7},{5,6},{6,5},{7,4},{8,11},{9,10},{10,... | collective-permute-start | bytes 344072 | tf_op jit(solution)/shard_map/ppermute | solution.py:441
  24.2 3.6 %collective-permute-done.5 = f32[4,56,128]{2,1,0:T(8,128)S(1)} collective-permute-done((f32[4,56,128]{2,1,0:T(8,128)S(1)}, f32[4,56,128]{2,1,0:T(8,128)S(1)}, u32[]{:S(2)}, u32[]{:S(2)}) %collective-permute-start.5) | collective-permute-done | bytes 114720 | tf_op jit(solution)/shard_map/ppermute | solution.py:441
  27.8 1.5 %collective-permute-start.6 = (f32[2,56,128]{2,1,0:T(8,128)S(1)}, f32[2,56,128]{2,1,0:T(8,128)S(1)}, u32[]{:S(2)}, u32[]{:S(2)}) collective-permute-start(f32[2,56,128]{2,1,0:T(8,128)S(1)} %get-tuple-element.22), channel_id=1, source_target_pairs={{0,5},{1,4},{2,7},{3,6},{4,1},{5,0},{6,3},{7,2},{8,13},{9,12},{10,... | collective-permute-start | bytes 172040 | tf_op jit(solution)/shard_map/ppermute | solution.py:441
  29.3 2.5 %collective-permute-done.6 = f32[2,56,128]{2,1,0:T(8,128)S(1)} collective-permute-done((f32[2,56,128]{2,1,0:T(8,128)S(1)}, f32[2,56,128]{2,1,0:T(8,128)S(1)}, u32[]{:S(2)}, u32[]{:S(2)}) %collective-permute-start.6) | collective-permute-done | bytes 57376 | tf_op jit(solution)/shard_map/ppermute | solution.py:441
  31.7 2.3 %collective-permute-start.7 = (f32[1,56,128]{2,1,0:T(8,128)S(1)}, f32[1,56,128]{2,1,0:T(8,128)S(1)}, u32[]{:S(2)}, u32[]{:S(2)}) collective-permute-start(f32[1,56,128]{2,1,0:T(8,128)S(1)} %get-tuple-element.23), channel_id=1, source_target_pairs={{0,9},{1,8},{2,11},{3,10},{4,13},{5,12},{6,15},{7,14},{8,1},{9,0},... | collective-permute-start | bytes 86024 | tf_op jit(solution)/shard_map/ppermute | solution.py:444
  34.0 1.9 %collective-permute-done.7.other_ref = f32[1,56,128]{2,1,0:T(8,128)S(1)} collective-permute-done((f32[1,56,128]{2,1,0:T(8,128)S(1)}, f32[1,56,128]{2,1,0:T(8,128)S(1)}, u32[]{:S(2)}, u32[]{:S(2)}) %collective-permute-start.7) | collective-permute-done | bytes 28704 | tf_op jit(solution)/shard_map/ppermute | solution.py:444
  36.0 0.0 copy-done.1
  36.0 0.0 copy-done.2
  36.0 0.9 %brick.1 = f32[1,4,2304]{2,1,0:T(4,128)} custom-call(f32[1,56,128]{2,1,0:T(8,128)S(1)} %get-tuple-element.24.mine_ref, f32[1,56,128]{2,1,0:T(8,128)S(1)} %collective-permute-done.7.other_ref, f32[4,640]{1,0:T(4,128)S(1)} %copy-done.1, f32[4,640]{1,0:T(4,128)S(1)} %copy-done.2), custom_call_target="tpu_custom_call" | custom-call | tf_op jit(solution)/shard_map/brick/pallas_call | solution.py:389
  (7 shorter events, 0.0 us)
Async XLA Ops:
  5.7 16.1 %copy-start = (f32[16,56,128]{2,1,0:T(8,128)S(1)}, f32[16,56,128]{2,1,0:T(8,128)}, u32[]{:S(2)}) copy-start(f32[16,56,128]{2,1,0:T(8,128)} %constant.6.clone.window_ref) | copy-start | bytes 1376260
  5.7 30.3 %copy-start.1 = (f32[4,640]{1,0:T(4,128)S(1)}, f32[4,640]{1,0:T(4,128)}, u32[]{:S(2)}) copy-start(f32[4,640]{1,0:T(4,128)} %constant.7.clone.rows_ref) | copy-start | bytes 30724
  5.7 30.3 %copy-start.2 = (f32[4,640]{1,0:T(4,128)S(1)}, f32[4,640]{1,0:T(4,128)}, u32[]{:S(2)}) copy-start(f32[4,640]{1,0:T(4,128)} %constant.8.clone.cols_ref) | copy-start | bytes 30724
  8.4 13.4 %collective-permute-start.4 = (f32[16,56,128]{2,1,0:T(8,128)S(1)}, f32[16,56,128]{2,1,0:T(8,128)S(1)}, u32[]{:S(2)}, u32[]{:S(2)}) collective-permute-start(f32[16,56,128]{2,1,0:T(8,128)S(1)} %shard_map.110.mine_ref), channel_id=1, source_target_pairs={{0,1},{1,0},{2,3},{3,2},{4,5},{5,4},{6,7},{7,6},{8,9},{9,8},{10,11... | collective-permute-start | bytes 1376264 | tf_op jit(solution)/shard_map/ppermute | solution.py:438
  9.6 4.0 %collective-permute-start = (s32[1,128]{1,0:T(1,128)S(1)}, s32[1,128]{1,0:T(1,128)S(1)}, u32[]{:S(2)}, u32[]{:S(2)}) collective-permute-start(s32[1,128]{1,0:T(1,128)S(1)} %seed.1), channel_id=1, source_target_pairs={{0,3},{1,2},{2,1},{3,0},{4,7},{5,6},{6,5},{7,4},{8,11},{9,10},{10,... | collective-permute-start | bytes 1544 | tf_op jit(solution)/shard_map/ppermute | solution.py:429
  13.6 3.0 %collective-permute-start.1 = (s32[1,128]{1,0:T(1,128)S(1)}, s32[1,128]{1,0:T(1,128)S(1)}, u32[]{:S(2)}, u32[]{:S(2)}) collective-permute-start(s32[1,128]{1,0:T(1,128)S(1)} %add.24), channel_id=1, source_target_pairs={{0,5},{1,4},{2,7},{3,6},{4,1},{5,0},{6,3},{7,2},{8,13},{9,12},{10,... | collective-permute-start | bytes 1544 | tf_op jit(solution)/shard_map/ppermute | solution.py:429
  16.6 4.0 %collective-permute-start.2 = (s32[1,128]{1,0:T(1,128)S(1)}, s32[1,128]{1,0:T(1,128)S(1)}, u32[]{:S(2)}, u32[]{:S(2)}) collective-permute-start(s32[1,128]{1,0:T(1,128)S(1)} %add.25), channel_id=1, source_target_pairs={{0,9},{1,8},{2,11},{3,10},{4,13},{5,12},{6,15},{7,14},{8,1},{9,0},... | collective-permute-start | bytes 1544 | tf_op jit(solution)/shard_map/ppermute | solution.py:429
  20.6 1.2 %collective-permute-start.3 = (s32[1,128]{1,0:T(1,128)S(1)}, s32[1,128]{1,0:T(1,128)S(1)}, u32[]{:S(2)}, u32[]{:S(2)}) collective-permute-start(s32[1,128]{1,0:T(1,128)S(1)} %add.26), channel_id=1, source_target_pairs={{0,1},{1,0},{2,3},{3,2},{4,5},{5,4},{6,7},{7,6},{8,9},{9,8},{10,11... | collective-permute-start | bytes 1544 | tf_op jit(solution)/shard_map/ppermute | solution.py:429
  22.6 5.2 %collective-permute-start.5 = (f32[4,56,128]{2,1,0:T(8,128)S(1)}, f32[4,56,128]{2,1,0:T(8,128)S(1)}, u32[]{:S(2)}, u32[]{:S(2)}) collective-permute-start(f32[4,56,128]{2,1,0:T(8,128)S(1)} %get-tuple-element.20), channel_id=1, source_target_pairs={{0,3},{1,2},{2,1},{3,0},{4,7},{5,6},{6,5},{7,4},{8,11},{9,10},{10,... | collective-permute-start | bytes 344072 | tf_op jit(solution)/shard_map/ppermute | solution.py:441
  27.8 3.9 %collective-permute-start.6 = (f32[2,56,128]{2,1,0:T(8,128)S(1)}, f32[2,56,128]{2,1,0:T(8,128)S(1)}, u32[]{:S(2)}, u32[]{:S(2)}) collective-permute-start(f32[2,56,128]{2,1,0:T(8,128)S(1)} %get-tuple-element.22), channel_id=1, source_target_pairs={{0,5},{1,4},{2,7},{3,6},{4,1},{5,0},{6,3},{7,2},{8,13},{9,12},{10,... | collective-permute-start | bytes 172040 | tf_op jit(solution)/shard_map/ppermute | solution.py:441
  31.7 4.3 %collective-permute-start.7 = (f32[1,56,128]{2,1,0:T(8,128)S(1)}, f32[1,56,128]{2,1,0:T(8,128)S(1)}, u32[]{:S(2)}, u32[]{:S(2)}) collective-permute-start(f32[1,56,128]{2,1,0:T(8,128)S(1)} %get-tuple-element.23), channel_id=1, source_target_pairs={{0,9},{1,8},{2,11},{3,10},{4,13},{5,12},{6,15},{7,14},{8,1},{9,0},... | collective-permute-start | bytes 86024 | tf_op jit(solution)/shard_map/ppermute | solution.py:444
where the time goes:
time: 37.1 us; the launch traced here: 36.9 us
  starting transfers between devices  13.1 us (35%)
  waiting for transfers between devices  12.4 us (33%)
  Pallas kernels  9.33 us (25%)
  between operations  2.04 us (5%)
    ppermute x4, starting transfers between devices, on_device(): got = lax.ppermute(tables[-1], 'patch', partner(devices, bit))  7.15 us
    ppermute x2, waiting for transfers between devices, on_device(): got = lax.ppermute(send, 'patch', partner(devices, bit))  6.01 us
    pallas_call x2, Pallas kernels, patch_half(): pl.pallas_call(functools.partial(patch_kernel, half, tiles, brick_rows, l...  5.67 us
    ppermute x4, waiting for transfers between devices, on_device(): got = lax.ppermute(tables[-1], 'patch', partner(devices, bit))  4.39 us
    ppermute x2, starting transfers between devices, on_device(): got = lax.ppermute(send, 'patch', partner(devices, bit))  3.08 us
    ppermute x1, starting transfers between devices, on_device(): other = lax.ppermute(send, 'patch', partner(devices, bits[-1]))  2.32 us
    pallas_call x1, Pallas kernels, front(): pl.pallas_call(functools.partial(front_kernel, math.isqrt(cells)), out_sh...  1.98 us
    ppermute x1, waiting for transfers between devices, on_device(): other = lax.ppermute(send, 'patch', partner(devices, bits[-1]))  1.94 us
  transfers between devices with their start and end apart: 8, of which 7 were waited for; matrix products, arithmetic and copies ran while one was open for 0% of the time, Pallas kernels for 0%

commit v1 on v0

--- a/solution.py
+++ b/solution.py
@@ -16,6 +16,7 @@
 I32 = jnp.int32
 PAD = 32
 LANES = 128
+CHUNKS = 3
 SPARE = 96
 
 
@@ -53,11 +54,16 @@
 
 
 def front_kernel(half, aug_ref, w_in_hbm, w_plane_hbm, w_depth_hbm, w_head_hbm, x_hbm, plane_ref, depth_ref, head_ref, xs_ref, w_in_ref, w_plane_ref, w_depth_ref, w_head_ref, x_ref, big_ref, plane_scr, depth_scr, sems):
-    pairs = ((w_plane_hbm, w_plane_ref), (w_in_hbm, w_in_ref), (w_depth_hbm, w_depth_ref), (w_head_hbm, w_head_ref), (x_hbm, x_ref))
+    size = x_hbm.shape[2] // CHUNKS
+    feats = [
+        pltpu.make_async_copy(x_hbm.at[:, :, pl.ds(c * size, size)], x_ref.at[:, :, pl.ds(c * size, size)], sems.at[4 + c])
+        for c in range(CHUNKS)
+    ]
+    pairs = ((w_plane_hbm, w_plane_ref), (w_in_hbm, w_in_ref), (w_depth_hbm, w_depth_ref), (w_head_hbm, w_head_ref))
     copies = [pltpu.make_async_copy(src, dst, sems.at[k]) for k, (src, dst) in enumerate(pairs)]
+    for copy in copies + feats:
+        copy.start()
     for copy in copies:
-        copy.start()
-    for copy in copies[:-1]:
         copy.wait()
     hidden, _ = w_in_ref.shape
     depth = depth_ref.shape[0] // PAD
@@ -108,24 +114,32 @@
     flip = (2 * yf + xf) * depth + (depth - 1) * zf
     head_ref[...] = jnp.where(at == (came ^ flip), wide, 0.0).astype(BF16)
 
-    copies[-1].wait()
     channels, depth, cells = x_ref.shape
     rows = depth * PAD
     margin = LANES
-    x = x_ref[...].reshape(channels * depth, cells)
-    projected = jnp.dot(big_ref[...], x, preferred_element_type=F32).astype(BF16)
     zeros = jnp.zeros((rows, margin), BF16)
-    padded = jnp.concatenate([zeros, projected, zeros], axis=1)
-    column = iota((rows, cells), 1) % half
     for d in range(3):
-        shifted = projected if d == 1 else lax.slice_in_dim(padded, margin + d - 1, margin + d - 1 + cells, axis=1)
-        if d == 0:
-            shifted = jnp.where(column == 0, jnp.zeros_like(shifted), shifted)
-        if d == 2:
-            shifted = jnp.where(column == half - 1, jnp.zeros_like(shifted), shifted)
         xs_ref[d, :, pl.ds(0, margin)] = zeros
-        xs_ref[d, :, pl.ds(margin, cells)] = shifted
         xs_ref[d, :, pl.ds(margin + cells, margin)] = zeros
+    size = cells // CHUNKS
+    column = iota((rows, size), 1)
+
+    def shift(c, d):
+        at = c * size
+        block = xs_ref[1, :, pl.ds(at, size + 2 * margin)]
+        moved = lax.slice_in_dim(block, margin + d - 1, margin + d - 1 + size, axis=1)
+        edge = (column + at) % half == (0 if d == 0 else half - 1)
+        xs_ref[d, :, pl.ds(margin + at, size)] = jnp.where(edge, jnp.zeros_like(moved), moved)
+
+    for c in range(CHUNKS):
+        part = pl.ds(c * size, size)
+        feats[c].wait()
+        x = x_ref[:, :, part].reshape(channels * depth, size)
+        xs_ref[1, :, pl.ds(margin + c * size, size)] = jnp.dot(big_ref[...], x, preferred_element_type=F32).astype(BF16)
+        shift(c, 0)
+        if c > 0:
+            shift(c - 1, 2)
+    shift(CHUNKS - 1, 2)
 
 
 def front(aug_code, w_in, w_plane, w_depth, w_head, feat):
@@ -150,7 +164,7 @@
             pltpu.VMEM((depth * PAD, channels * depth), BF16),
             pltpu.VMEM(plane, F32),
             pltpu.VMEM(depth_w, F32),
-            pltpu.SemaphoreType.DMA((5,)),
+            pltpu.SemaphoreType.DMA((4 + CHUNKS,)),
         ],
         compiler_params=params(),
         cost_estimate=cost(10**8),
@@ -158,39 +172,46 @@
     )(aug_code, *stay(w_in, w_plane, w_depth, w_head, feat))
 
 
-def patch_kernel(half, tiles, brick_rows, last, aug_ref, xs_ref, plane_ref, depth_ref, head_ref, *refs):
+def patch_kernel(half, tiles, brick_rows, keep_from, last, aug_ref, xs_ref, plane_ref, depth_ref, head_ref, *refs):
     if last:
-        carry_in, _, out_ref, a_ref = refs
+        carry_in, _, anchor_ref, out_ref, anchor_out, a_ref = refs
+        anchor_out[...] = jnp.full(anchor_out.shape, anchor_ref[0], I32)
     else:
         out_ref, carry_out, a_ref = refs
     _, rows, _ = xs_ref.shape
     depth = rows // PAD
     step = 2 * LANES
     margin = LANES
-    first_tile = tiles[0] * (step // LANES) - (1 if last else 0)
+    carried = carry_in.shape[0] if last else 0
+    first_tile = tiles[0] * (step // LANES) - carried
     if last:
-        a_ref[0] = carry_in[...]
-
-    for t in tiles:
+        a_ref[pl.ds(0, carried)] = carry_in[...]
+
+    def window_stage(t):
         near = []
         for d in range(3):
             block = xs_ref[d, :, pl.ds(t * step, step + 2 * margin)]
             near.append([lax.slice_in_dim(block, margin + half * e, margin + half * e + step, axis=1) for e in (-1, 0, 1)])
-        centre = near[1][1].astype(F32)
-        first = [[None] * depth for _ in range(4)]
-        for z in range(depth):
-            cut = slice(z * PAD, (z + 1) * PAD)
-            for py in range(2):
-                around = jnp.concatenate([near[d][py + e][cut] for e in range(2) for d in range(3)], axis=0)
-                mix = jnp.dot(plane_ref[py], around, preferred_element_type=F32)
-                for px in range(2):
-                    total = mix[px * PAD : (px + 1) * PAD] + mix[(2 + px) * PAD : (3 + px) * PAD]
-                    first[2 * py + px][z] = (centre[cut] + jnp.maximum(total, 0.0)).astype(BF16)
-        second = []
-        for p in range(4):
-            one = jnp.concatenate(first[p], axis=0)
-            mix = jnp.dot(depth_ref[...], one, preferred_element_type=F32)
-            second.append((one.astype(F32) + jnp.maximum(mix, 0.0)).astype(BF16))
+        return near
+
+    def plane_stage(near, z):
+        cut = slice(z * PAD, (z + 1) * PAD)
+        centre = near[1][1][cut].astype(F32)
+        first = []
+        for py in range(2):
+            around = jnp.concatenate([near[d][py + e][cut] for e in range(2) for d in range(3)], axis=0)
+            mix = jnp.dot(plane_ref[py], around, preferred_element_type=F32)
+            for px in range(2):
+                total = mix[px * PAD : (px + 1) * PAD] + mix[(2 + px) * PAD : (3 + px) * PAD]
+                first.append((centre + jnp.maximum(total, 0.0)).astype(BF16))
+        return first
+
+    def depth_stage(first, p):
+        one = jnp.concatenate([first[z][p] for z in range(depth)], axis=0)
+        mix = jnp.dot(depth_ref[...], one, preferred_element_type=F32)
+        return (one.astype(F32) + jnp.maximum(mix, 0.0)).astype(BF16)
+
+    def head_stage(t, second):
         logits = jnp.zeros((head_ref.shape[0], step), F32)
         for q in range(2):
             pair = jnp.concatenate(second[2 * q : 2 * q + 2], axis=0)
@@ -199,62 +220,86 @@
         for u in range(step // LANES):
             a_ref[t * (step // LANES) + u - first_tile] = affinity[:, u * LANES : (u + 1) * LANES]
 
-    if not last:
-        carry_out[...] = a_ref[(tiles[-1] + 1) * (step // LANES) - 1 - first_tile]
-
     aug = aug_ref[0]
     yf, xf = (aug >> 1) & 1, (aug >> 2) & 1
-
     side = half // 4
     tail = side * side - LANES
     row_tiles = head_ref.shape[0] // 8
     lane = iota((8, LANES), 1)
+    group = lane // tail
+    span = -(-side * half // LANES)
+    near_tiles = span - 2
 
     def source(cell, j, odd):
-        yl = cell // side
-        xl = cell - yl * side
-        y = jnp.where(yf == 1, side - 1 - yl, yl)
-        xx = side * j + xl
-        xx = jnp.where(xf == 1, half - 1 - xx, xx)
-        return y * half + xx + odd * (LANES // 2)
-
-    span = -(-side * half // LANES)
-    rest_base = jnp.where(yf == 1, 0, span - 2)
-    group = lane // tail
-    for odd in range(2):
-        for j in range(4):
-            src = source(lane, j, odd)
-            tile_of, lane_of = src // LANES, src % LANES
-            hits = [tile_of == k for k in range(span)]
-            rest = source(LANES + lane % tail, j, odd)
-            rest_hit = rest // LANES == rest_base
-            rest_lane = rest % LANES
-            for i in [k for k in brick_rows if k % 2 == odd]:
-                base = side * half * i // LANES - first_tile
-                brick = (i ^ (3 * yf)) * 4 + j
-                packed = jnp.zeros((8, LANES), F32)
-                for r in range(row_tiles):
-                    cut = pl.ds(8 * r, 8)
-                    value = jnp.take_along_axis(a_ref[base, cut], lane_of, axis=1)
-                    for k in range(1, span):
-                        value = jnp.where(hits[k], jnp.take_along_axis(a_ref[base + k, cut], lane_of, axis=1), value)
-                    out_ref[brick, cut] = value
-                    low = jnp.take_along_axis(a_ref[base + rest_base, cut], rest_lane, axis=1)
-                    high = jnp.take_along_axis(a_ref[base + rest_base + 1, cut], rest_lane, axis=1)
-                    packed = jnp.where(group == r, jnp.where(rest_hit, low, high), packed)
-                out_ref[brick, pl.ds(8 * row_tiles, 8)] = packed
-
-
-def patch_half(half, tiles, brick_rows, last, aug_code, shifted, plane, depth_w, head, extra=()):
+        y = cell // side
+        x = cell - y * side
+        y = jnp.where(yf == 1, side - 1 - y, y)
+        x = jnp.where(xf == 1, side - 1 - x, x)
+        return y * half + side * j + x + odd * (LANES // 2)
+
+    def cut_stage(i, j):
+        odd = i % 2
+        owned = []
+        for k in range(span):
+            x = (lane + k * LANES + half - odd * (LANES // 2) % half) % half
+            owned.append((x >= side * j) & (x < side * (j + 1)))
+        src = source(lane, j, odd)
+        main_lane, main_near = src % LANES, src < near_tiles * LANES
+        rest_lane = source(LANES + lane % tail, j, odd) % LANES
+        base = side * half * i // LANES - first_tile
+        brick = (i ^ (3 * yf)) * 4 + (j ^ (3 * xf))
+        packed = jnp.zeros((8, LANES), F32)
+        for r in range(row_tiles):
+            cut = pl.ds(8 * r, 8)
+            merged = []
+            for tiles_of in (range(near_tiles), range(near_tiles, span)):
+                one = a_ref[base + tiles_of[0], cut]
+                for k in tiles_of[1:]:
+                    one = jnp.where(owned[k], a_ref[base + k, cut], one)
+                merged.append(one)
+            low = jnp.take_along_axis(merged[0], main_lane, axis=1)
+            high = jnp.take_along_axis(merged[1], main_lane, axis=1)
+            out_ref[brick, cut] = jnp.where(main_near, low, high)
+            rest = jnp.take_along_axis(jnp.where(yf == 1, merged[0], merged[1]), rest_lane, axis=1)
+            packed = jnp.where(group == r, rest, packed)
+        out_ref[brick, pl.ds(8 * row_tiles, 8)] = packed
+
+    first, second = {}, {}
+    waiting = [(i, j) for i in brick_rows for j in range(4)]
+    done = first_tile + carried
+    for k in range(len(tiles) + 2):
+        if k < len(tiles):
+            near = window_stage(tiles[k])
+            first[k] = []
+        second[k - 1] = []
+        for q in range(4):
+            if k < len(tiles) and q < depth:
+                first[k].append(plane_stage(near, q))
+            if 0 <= k - 1 < len(tiles):
+                second[k - 1].append(depth_stage(first[k - 1], q))
+            if waiting and done >= side * half * waiting[0][0] // LANES + span:
+                cut_stage(*waiting.pop(0))
+        if 0 <= k - 2 < len(tiles):
+            head_stage(tiles[k - 2], second[k - 2])
+            done += step // LANES
+    for left in waiting:
+        cut_stage(*left)
+    if not last:
+        carry_out[...] = a_ref[pl.ds(keep_from - first_tile, done - keep_from)]
+
+
+def patch_half(half, tiles, brick_rows, keep_from, last, aug_code, shifted, plane, depth_w, head, extra=()):
     kept = head.shape[0]
+    carried = extra[0].shape[0] if last else 0
     bricks = jax.ShapeDtypeStruct((16, kept + 8, LANES), F32)
-    carry = jax.ShapeDtypeStruct((kept, LANES), F32)
+    beside = jax.ShapeDtypeStruct((1, LANES), I32) if last else jax.ShapeDtypeStruct((2 * len(tiles) - keep_from, kept, LANES), F32)
+    spaces = [vmem(), vmem(), smem()] if last else []
     return pl.pallas_call(
-        functools.partial(patch_kernel, half, tiles, brick_rows, last),
-        out_shape=[bricks] if last else [bricks, carry],
-        in_specs=[smem()] + [vmem()] * (4 + len(extra)),
-        out_specs=[vmem()] if last else [vmem()] * 2,
-        scratch_shapes=[pltpu.VMEM((2 * len(tiles) + 1, kept, LANES), F32)],
+        functools.partial(patch_kernel, half, tiles, brick_rows, keep_from, last),
+        out_shape=[bricks, beside],
+        in_specs=[smem()] + [vmem()] * 4 + spaces,
+        out_specs=[vmem()] * 2,
+        scratch_shapes=[pltpu.VMEM((2 * len(tiles) + carried, kept, LANES), F32)],
         input_output_aliases={6: 0} if last else {},
         compiler_params=params(),
         cost_estimate=cost(10**9),
@@ -291,7 +336,7 @@
         return 0
 
     lax.fori_loop(0, devices, note, 0)
-    anchor = anchor_ref[0]
+    anchor = anchor_ref[0, 0]
     count = 1 << len(bits)
     _, rows, lanes = mine_ref.shape
     spare = iota((rows, lanes), 1) - jnp.where(iota((rows, lanes), 0) == rows - 8, SPARE, lanes)
@@ -326,13 +371,13 @@
     )(table, anchor, mine, other, window)
 
 
-def brick_kernel(side, maps, depth_curve, mine_ref, other_ref, rows_ref, cols_ref, out_ref):
+def brick_kernel(side, maps, depth_curve, mine_ref, a_ref, b_ref, c_ref, rows_ref, cols_ref, out_ref):
     depth = len(depth_curve)
     wide = 2 * side
     plane = wide * wide
     tail = side * side - LANES
     per = depth * maps
-    brick = mine_ref[0] + other_ref[0]
+    brick = (mine_ref[0] + a_ref[0]) + (b_ref[0] + c_ref[0])
     kept = 4 * per
     main, packed = brick[:kept], brick[kept:]
     rest = jnp.concatenate([packed if k == 0 else pltpu.roll(packed, LANES - tail * k, 1) for k in range(kept // 8)], axis=0)
@@ -377,7 +422,7 @@
         out_ref[0, pl.ds(maps, 1), pl.ds(z * plane, plane)] = window * depth_curve[z]
 
 
-def finish(side, maps, depth, mine, other):
+def finish(side, maps, depth, mine, others):
     plane = 4 * side * side
     width = -(-plane // LANES) * LANES
     curve = bump(8 * side)
@@ -389,11 +434,11 @@
     return pl.pallas_call(
         functools.partial(brick_kernel, side, maps, depth_curve),
         out_shape=jax.ShapeDtypeStruct((1, maps + 1, depth * plane), F32),
-        in_specs=[vmem()] * 4,
+        in_specs=[vmem()] * 6,
         out_specs=vmem(),
         compiler_params=params(),
         name="brick",
-    )(mine, other, rows, cols)
+    )(mine, *others, rows, cols)
 
 
 def wire_window(side, maps, depth):
@@ -421,11 +466,13 @@
     _, _, depth, cells = features.shape
     side = math.isqrt(cells) // 4
     maps = w_head.shape[0]
-    bits = [1] + [1 << k | 1 for k in range(1, devices.bit_length() - 1)]
+    levels = [1 << k for k in range(devices.bit_length() - 1)]
+    paired = levels[:1] + [bit | 1 for bit in levels[1:]]
+    bits = paired[1:-2] + [levels[-2], paired[-1]]
 
     table = seed_table(brick_owner, devices)
     tables = [table]
-    for bit in bits[1:] + bits[:1]:
+    for bit in paired[1:] + paired[:1]:
         got = lax.ppermute(tables[-1], "patch", partner(devices, bit))
         tables.append(tables[-1] + got)
     table = tables[-1]
@@ -433,16 +480,24 @@
     half = math.isqrt(cells)
     steps = cells // (2 * LANES)
     ready = -(-half * half // 2 // (2 * LANES))
-    bricks, carry = patch_half(half, range(ready), (0, 1), False, aug_code, shifted, plane, depth_w, head)
-    (bricks,) = patch_half(half, range(ready, steps), (2, 3), True, aug_code, shifted, plane, depth_w, head, (carry, bricks))
+    quarter = half * half // 4 // LANES
+    bricks, carry = patch_half(half, range(ready), (0,), quarter, False, aug_code, shifted, plane, depth_w, head)
+    bricks, anchor = patch_half(
+        half, range(ready, steps), (1, 2, 3), 0, True, aug_code, shifted, plane, depth_w, head, (carry, bricks, patch_anchor)
+    )
     other = lax.ppermute(bricks, "patch", partner(devices, 1))
-    send, keep = fill_slots(devices, bits[1:], table, patch_anchor, bricks, other, wire_window(side, maps, depth))
-    for bit in bits[1:-1]:
+    send, keep = fill_slots(devices, bits, table, anchor, bricks, other, wire_window(side, maps, depth))
+    for bit in bits[:-2]:
         got = lax.ppermute(send, "patch", partner(devices, bit))
         half = send.shape[0] // 2
-        keep, send = keep[:half] + got[:half], keep[half:] + got[half:]
-    other = lax.ppermute(send, "patch", partner(devices, bits[-1]))
-    return finish(side, maps, depth, keep, other)
+        last = half == 2
+        cuts = [slice(k, k + 1) for k in range(4)] if last else [slice(0, half), slice(half, 2 * half)]
+        parts = [keep[c] + got[c] for c in cuts]
+        if not last:
+            keep, send = parts
+    far = [bits[-1], bits[-2], bits[-1] ^ bits[-2]]
+    others = [lax.ppermute(part, "patch", partner(devices, bit)) for part, bit in zip(parts[1:], far)]
+    return finish(side, maps, depth, parts[0], others)
 
 
 def solution(mesh):

time: 37.1 us -> 37.8 us (1.019)
  waiting for transfers between devices: 12.4 us -> 13.9 us
  Pallas kernels: 9.33 us -> 8.28 us
    ppermute x1 -> x3, waiting for transfers between devices: 1.94 us -> 5.33 us  [on_device(): lax.ppermute(part, 'patch', partner(devices, bit))]
    ppermute x2 -> x1, waiting for transfers between devices: 6.01 us -> 3.57 us  [on_device(): got = lax.ppermute(send, 'patch', partner(devices, bit))]
    ppermute x1 -> x3, starting transfers between devices: 2.32 us -> 4.07 us  [on_device(): lax.ppermute(part, 'patch', partner(devices, bit))]
    ppermute x2 -> x1, starting transfers between devices: 3.08 us -> 1.59 us  [on_device(): got = lax.ppermute(send, 'patch', partner(devices, bit))]
    pallas_call x2, Pallas kernels: 5.67 us -> 4.3 us  [patch_half(): pl.pallas_call(functools.partial(patch_kernel, half, tiles, brick_rows, k...]
    ppermute x4, waiting for transfers between devices: 4.39 us -> 5.04 us  [on_device(): got = lax.ppermute(tables[-1], 'patch', partner(devices, bit))]
  transfers between devices with their start and end apart: 8 -> 9, of which waited for: 7 -> 8; matrix products, arithmetic and copies ran while one was open for 0% -> 0% of each run, Pallas kernels for 0% -> 0%
where the time goes in v1:
time: 37.8 us; the launch traced here: 37.7 us
  waiting for transfers between devices  13.9 us (37%)
  starting transfers between devices  13.4 us (35%)
  Pallas kernels  8.28 us (22%)
  between operations  2.03 us (5%)
    ppermute x4, starting transfers between devices, on_device(): got = lax.ppermute(tables[-1], 'patch', partner(devices, bit))  7.15 us
    ppermute x3, waiting for transfers between devices, on_device(): lax.ppermute(part, 'patch', partner(devices, bit))  5.33 us
    ppermute x4, waiting for transfers between devices, on_device(): got = lax.ppermute(tables[-1], 'patch', partner(devices, bit))  5.04 us
    pallas_call x2, Pallas kernels, patch_half(): pl.pallas_call(functools.partial(patch_kernel, half, tiles, brick_rows, k...  4.3 us
    ppermute x3, starting transfers between devices, on_device(): lax.ppermute(part, 'patch', partner(devices, bit))  4.07 us
    ppermute x1, waiting for transfers between devices, on_device(): got = lax.ppermute(send, 'patch', partner(devices, bit))  3.57 us
    pallas_call x1, Pallas kernels, front(): pl.pallas_call(functools.partial(front_kernel, math.isqrt(cells)), out_sh...  2.3 us
    ppermute x1, starting transfers between devices, on_device(): got = lax.ppermute(send, 'patch', partner(devices, bit))  1.59 us
  transfers between devices with their start and end apart: 9, of which 8 were waited for; matrix products, arithmetic and copies ran while one was open for 0% of the time, Pallas kernels for 0%

profile of v1, /device:TPU:0, one launch (start us, length us, event | category | flops | bytes accessed | tf_op | source)
XLA Modules:
  0.0 37.7 jit_solution(16612977556733504172)
XLA Ops:
  1.3 2.3 %front.1 = (bf16[2,128,192]{2,1,0:T(8,128)(2,1)S(1)}, bf16[128,128]{1,0:T(8,128)(2,1)S(1)}, bf16[48,512]{1,0:T(8,128)(2,1)S(1)}, bf16[3,128,2560]{2,1,0:T(8,128)(2,1)S(1)}) custom-call(s32[1]{0:T(128)S(6)} %copy.16.aug_ref, bf16[28,64]{1,0:T(8,128)(2,1)} %w_in_hbm.1, bf16[9,28,28]{2,1,0:T(8,128)(2,1)} %w_plane_hbm.1, bf16[3,28,28]{2,1,0:T(8,128)(2,1)} %w_depth_hbm.1, ...), custom_call_target="tpu_custom_call" | custom-call | flops 100000000 | bytes 1048576 | tf_op jit(solution)/shard_map/front/pallas_call | solution.py:153
  3.6 2.3 %shard_map.109 = (f32[16,56,128]{2,1,0:T(8,128)S(1)}, f32[6,48,128]{2,1,0:T(8,128)S(1)}) custom-call(s32[1]{0:T(128)S(6)} %copy.16.aug_ref, bf16[3,128,2560]{2,1,0:T(8,128)(2,1)S(1)} %get-tuple-element.15.xs_ref, bf16[2,128,192]{2,1,0:T(8,128)(2,1)S(1)} %get-tuple-element.16.plane_ref, bf16[128,128]{1,0:T(8,128)(2,1)S(1)} %get-tuple-element.17.depth_ref, ...), custom_call_target="tpu_custom_call" | custom-call | flops 1000000000 | bytes 1048576 | tf_op jit(solution)/shard_map/pallas_call | solution.py:297
  5.9 0.0 copy-start
  5.9 0.0 copy-start.1
  5.9 0.0 copy-start.2
  5.9 2.0 %shard_map.110 = (f32[16,56,128]{2,1,0:T(8,128)S(1)}, s32[1,128]{1,0:T(1,128)S(1)}) custom-call(s32[1]{0:T(128)S(6)} %copy.16.aug_ref, bf16[3,128,2560]{2,1,0:T(8,128)(2,1)S(1)} %get-tuple-element.15.xs_ref, bf16[2,128,192]{2,1,0:T(8,128)(2,1)S(1)} %get-tuple-element.16.plane_ref, ...), custom_call_target="tpu_custom_call", output_to_operand_aliasing={{0}: (6, {})} | custom-call | flops 1000000000 | bytes 1048576 | tf_op jit(solution)/shard_map/pallas_call | solution.py:297
  8.0 0.6 %collective-permute-start.4 = (f32[16,56,128]{2,1,0:T(8,128)S(1)}, f32[16,56,128]{2,1,0:T(8,128)S(1)}, u32[]{:S(2)}, u32[]{:S(2)}) collective-permute-start(f32[16,56,128]{2,1,0:T(8,128)S(1)} %get-tuple-element.22.mine_ref), channel_id=1, source_target_pairs={{0,1},{1,0},{2,3},{3,2},{4,5},{5,4},{6,7},{7,6},{8,9},{9,8},{10,11... | collective-permute-start | bytes 1376264 | tf_op jit(solution)/shard_map/ppermute | solution.py:488
  9.2 2.7 %collective-permute-start = (s32[1,128]{1,0:T(1,128)S(1)}, s32[1,128]{1,0:T(1,128)S(1)}, u32[]{:S(2)}, u32[]{:S(2)}) collective-permute-start(s32[1,128]{1,0:T(1,128)S(1)} %seed.1), channel_id=1, source_target_pairs={{0,3},{1,2},{2,1},{3,0},{4,7},{5,6},{6,5},{7,4},{8,11},{9,10},{10,... | collective-permute-start | bytes 1544 | tf_op jit(solution)/shard_map/ppermute | solution.py:476
  11.9 1.3 %collective-permute-done = s32[1,128]{1,0:T(1,128)S(1)} collective-permute-done((s32[1,128]{1,0:T(1,128)S(1)}, s32[1,128]{1,0:T(1,128)S(1)}, u32[]{:S(2)}, u32[]{:S(2)}) %collective-permute-start) | collective-permute-done | bytes 544 | tf_op jit(solution)/shard_map/ppermute | solution.py:476
  13.2 1.7 %collective-permute-start.1 = (s32[1,128]{1,0:T(1,128)S(1)}, s32[1,128]{1,0:T(1,128)S(1)}, u32[]{:S(2)}, u32[]{:S(2)}) collective-permute-start(s32[1,128]{1,0:T(1,128)S(1)} %add.24), channel_id=1, source_target_pairs={{0,5},{1,4},{2,7},{3,6},{4,1},{5,0},{6,3},{7,2},{8,13},{9,12},{10,... | collective-permute-start | bytes 1544 | tf_op jit(solution)/shard_map/ppermute | solution.py:476
  14.9 1.3 %collective-permute-done.1 = s32[1,128]{1,0:T(1,128)S(1)} collective-permute-done((s32[1,128]{1,0:T(1,128)S(1)}, s32[1,128]{1,0:T(1,128)S(1)}, u32[]{:S(2)}, u32[]{:S(2)}) %collective-permute-start.1) | collective-permute-done | bytes 544 | tf_op jit(solution)/shard_map/ppermute | solution.py:476
  16.2 2.7 %collective-permute-start.2 = (s32[1,128]{1,0:T(1,128)S(1)}, s32[1,128]{1,0:T(1,128)S(1)}, u32[]{:S(2)}, u32[]{:S(2)}) collective-permute-start(s32[1,128]{1,0:T(1,128)S(1)} %add.25), channel_id=1, source_target_pairs={{0,9},{1,8},{2,11},{3,10},{4,13},{5,12},{6,15},{7,14},{8,1},{9,0},... | collective-permute-start | bytes 1544 | tf_op jit(solution)/shard_map/ppermute | solution.py:476
  18.9 1.3 %collective-permute-done.2 = s32[1,128]{1,0:T(1,128)S(1)} collective-permute-done((s32[1,128]{1,0:T(1,128)S(1)}, s32[1,128]{1,0:T(1,128)S(1)}, u32[]{:S(2)}, u32[]{:S(2)}) %collective-permute-start.2) | collective-permute-done | bytes 544 | tf_op jit(solution)/shard_map/ppermute | solution.py:476
  20.2 0.0 collective-permute-start.3
  20.2 1.2 %collective-permute-done.3 = s32[1,128]{1,0:T(1,128)S(1)} collective-permute-done((s32[1,128]{1,0:T(1,128)S(1)}, s32[1,128]{1,0:T(1,128)S(1)}, u32[]{:S(2)}, u32[]{:S(2)}) %collective-permute-start.3) | collective-permute-done | bytes 544 | tf_op jit(solution)/shard_map/ppermute | solution.py:476
  21.4 0.0 collective-permute-done.4.other_ref
  21.4 0.0 copy-done
  21.4 0.8 %slots.1 = (f32[4,56,128]{2,1,0:T(8,128)S(1)}, f32[4,56,128]{2,1,0:T(8,128)S(1)}) custom-call(s32[1,128]{1,0:T(1,128)S(1)} %add.27.table_ref, s32[1,128]{1,0:T(1,128)S(1)} %get-tuple-element.21.anchor_ref, f32[16,56,128]{2,1,0:T(8,128)S(1)} %get-tuple-element.22.mine_ref, f32[16,56,128]{2,1,0:T(8,128)S(1)} %collective-permute-done.4.other_ref, ...), custom_call_target="tpu_custom_call" | custom-call | tf_op jit(solution)/shard_map/slots/pallas_call | solution.py:363
  22.2 1.6 %collective-permute-start.5 = (f32[4,56,128]{2,1,0:T(8,128)S(1)}, f32[4,56,128]{2,1,0:T(8,128)S(1)}, u32[]{:S(2)}, u32[]{:S(2)}) collective-permute-start(f32[4,56,128]{2,1,0:T(8,128)S(1)} %get-tuple-element.24), channel_id=1, source_target_pairs={{0,3},{1,2},{2,1},{3,0},{4,7},{5,6},{6,5},{7,4},{8,11},{9,10},{10,... | collective-permute-start | bytes 344072 | tf_op jit(solution)/shard_map/ppermute | solution.py:491
  23.8 3.6 %collective-permute-done.5 = f32[4,56,128]{2,1,0:T(8,128)S(1)} collective-permute-done((f32[4,56,128]{2,1,0:T(8,128)S(1)}, f32[4,56,128]{2,1,0:T(8,128)S(1)}, u32[]{:S(2)}, u32[]{:S(2)}) %collective-permute-start.5) | collective-permute-done | bytes 114720 | tf_op jit(solution)/shard_map/ppermute | solution.py:491
  27.4 2.5 %collective-permute-start.6 = (f32[1,56,128]{2,1,0:T(8,128)S(1)}, f32[1,56,128]{2,1,0:T(8,128)S(1)}, u32[]{:S(2)}, u32[]{:S(2)}) collective-permute-start(f32[1,56,128]{2,1,0:T(8,128)S(1)} %get-tuple-element.27), channel_id=1, source_target_pairs={{0,9},{1,8},{2,11},{3,10},{4,13},{5,12},{6,15},{7,14},{8,1},{9,0},... | collective-permute-start | bytes 86024 | tf_op jit(solution)/shard_map/ppermute | solution.py:499
  29.9 1.6 %collective-permute-start.7 = (f32[1,56,128]{2,1,0:T(8,128)S(1)}, f32[1,56,128]{2,1,0:T(8,128)S(1)}, u32[]{:S(2)}, u32[]{:S(2)}) collective-permute-start(f32[1,56,128]{2,1,0:T(8,128)S(1)} %get-tuple-element.26), channel_id=1, source_target_pairs={{0,4},{1,5},{2,6},{3,7},{4,0},{5,1},{6,2},{7,3},{8,12},{9,13},{10,... | collective-permute-start | bytes 86024 | tf_op jit(solution)/shard_map/ppermute | solution.py:499
  31.4 0.0 collective-permute-start.8
  31.5 0.2 collective-permute-done.6.a_ref
  31.6 2.1 %collective-permute-done.7.b_ref = f32[1,56,128]{2,1,0:T(8,128)S(1)} collective-permute-done((f32[1,56,128]{2,1,0:T(8,128)S(1)}, f32[1,56,128]{2,1,0:T(8,128)S(1)}, u32[]{:S(2)}, u32[]{:S(2)}) %collective-permute-start.7) | collective-permute-done | bytes 28704 | tf_op jit(solution)/shard_map/ppermute | solution.py:499
  33.7 3.0 %collective-permute-done.8.c_ref = f32[1,56,128]{2,1,0:T(8,128)S(1)} collective-permute-done((f32[1,56,128]{2,1,0:T(8,128)S(1)}, f32[1,56,128]{2,1,0:T(8,128)S(1)}, u32[]{:S(2)}, u32[]{:S(2)}) %collective-permute-start.8) | collective-permute-done | bytes 28704 | tf_op jit(solution)/shard_map/ppermute | solution.py:499
  36.8 0.0 copy-done.1
  36.8 0.0 copy-done.2
  36.8 0.9 %brick.1 = f32[1,4,2304]{2,1,0:T(4,128)} custom-call(f32[1,56,128]{2,1,0:T(8,128)S(1)} %get-tuple-element.28.mine_ref, f32[1,56,128]{2,1,0:T(8,128)S(1)} %collective-permute-done.6.a_ref, f32[1,56,128]{2,1,0:T(8,128)S(1)} %collective-permute-done.7.b_ref, f32[1,56,128]{2,1,0:T(8,128)S(1)} %collective-permute-done.8.c_ref, f32[4,640]{1,0:T(4,128)S(1)} %copy-done.1, ...), custom_call_target="tpu_custom_call" | custom-call | tf_op jit(solution)/shard_map/brick/pallas_call | solution.py:434
  (6 shorter events, 0.0 us)
Async XLA Ops:
  5.9 15.5 %copy-start = (f32[16,56,128]{2,1,0:T(8,128)S(1)}, f32[16,56,128]{2,1,0:T(8,128)}, u32[]{:S(2)}) copy-start(f32[16,56,128]{2,1,0:T(8,128)} %constant.6.clone.window_ref) | copy-start | bytes 1376260
  5.9 30.9 %copy-start.1 = (f32[4,640]{1,0:T(4,128)S(1)}, f32[4,640]{1,0:T(4,128)}, u32[]{:S(2)}) copy-start(f32[4,640]{1,0:T(4,128)} %constant.7.clone.rows_ref) | copy-start | bytes 30724
  5.9 30.9 %copy-start.2 = (f32[4,640]{1,0:T(4,128)S(1)}, f32[4,640]{1,0:T(4,128)}, u32[]{:S(2)}) copy-start(f32[4,640]{1,0:T(4,128)} %constant.8.clone.cols_ref) | copy-start | bytes 30724
  8.0 13.4 %collective-permute-start.4 = (f32[16,56,128]{2,1,0:T(8,128)S(1)}, f32[16,56,128]{2,1,0:T(8,128)S(1)}, u32[]{:S(2)}, u32[]{:S(2)}) collective-permute-start(f32[16,56,128]{2,1,0:T(8,128)S(1)} %get-tuple-element.22.mine_ref), channel_id=1, source_target_pairs={{0,1},{1,0},{2,3},{3,2},{4,5},{5,4},{6,7},{7,6},{8,9},{9,8},{10,11... | collective-permute-start | bytes 1376264 | tf_op jit(solution)/shard_map/ppermute | solution.py:488
  9.2 4.0 %collective-permute-start = (s32[1,128]{1,0:T(1,128)S(1)}, s32[1,128]{1,0:T(1,128)S(1)}, u32[]{:S(2)}, u32[]{:S(2)}) collective-permute-start(s32[1,128]{1,0:T(1,128)S(1)} %seed.1), channel_id=1, source_target_pairs={{0,3},{1,2},{2,1},{3,0},{4,7},{5,6},{6,5},{7,4},{8,11},{9,10},{10,... | collective-permute-start | bytes 1544 | tf_op jit(solution)/shard_map/ppermute | solution.py:476
  13.2 3.0 %collective-permute-start.1 = (s32[1,128]{1,0:T(1,128)S(1)}, s32[1,128]{1,0:T(1,128)S(1)}, u32[]{:S(2)}, u32[]{:S(2)}) collective-permute-start(s32[1,128]{1,0:T(1,128)S(1)} %add.24), channel_id=1, source_target_pairs={{0,5},{1,4},{2,7},{3,6},{4,1},{5,0},{6,3},{7,2},{8,13},{9,12},{10,... | collective-permute-start | bytes 1544 | tf_op jit(solution)/shard_map/ppermute | solution.py:476
  16.2 4.0 %collective-permute-start.2 = (s32[1,128]{1,0:T(1,128)S(1)}, s32[1,128]{1,0:T(1,128)S(1)}, u32[]{:S(2)}, u32[]{:S(2)}) collective-permute-start(s32[1,128]{1,0:T(1,128)S(1)} %add.25), channel_id=1, source_target_pairs={{0,9},{1,8},{2,11},{3,10},{4,13},{5,12},{6,15},{7,14},{8,1},{9,0},... | collective-permute-start | bytes 1544 | tf_op jit(solution)/shard_map/ppermute | solution.py:476
  20.2 1.2 %collective-permute-start.3 = (s32[1,128]{1,0:T(1,128)S(1)}, s32[1,128]{1,0:T(1,128)S(1)}, u32[]{:S(2)}, u32[]{:S(2)}) collective-permute-start(s32[1,128]{1,0:T(1,128)S(1)} %add.26), channel_id=1, source_target_pairs={{0,1},{1,0},{2,3},{3,2},{4,5},{5,4},{6,7},{7,6},{8,9},{9,8},{10,11... | collective-permute-start | bytes 1544 | tf_op jit(solution)/shard_map/ppermute | solution.py:476
  22.2 5.2 %collective-permute-start.5 = (f32[4,56,128]{2,1,0:T(8,128)S(1)}, f32[4,56,128]{2,1,0:T(8,128)S(1)}, u32[]{:S(2)}, u32[]{:S(2)}) collective-permute-start(f32[4,56,128]{2,1,0:T(8,128)S(1)} %get-tuple-element.24), channel_id=1, source_target_pairs={{0,3},{1,2},{2,1},{3,0},{4,7},{5,6},{6,5},{7,4},{8,11},{9,10},{10,... | collective-permute-start | bytes 344072 | tf_op jit(solution)/shard_map/ppermute | solution.py:491
  27.4 4.3 %collective-permute-start.6 = (f32[1,56,128]{2,1,0:T(8,128)S(1)}, f32[1,56,128]{2,1,0:T(8,128)S(1)}, u32[]{:S(2)}, u32[]{:S(2)}) collective-permute-start(f32[1,56,128]{2,1,0:T(8,128)S(1)} %get-tuple-element.27), channel_id=1, source_target_pairs={{0,9},{1,8},{2,11},{3,10},{4,13},{5,12},{6,15},{7,14},{8,1},{9,0},... | collective-permute-start | bytes 86024 | tf_op jit(solution)/shard_map/ppermute | solution.py:499
  29.9 3.9 %collective-permute-start.7 = (f32[1,56,128]{2,1,0:T(8,128)S(1)}, f32[1,56,128]{2,1,0:T(8,128)S(1)}, u32[]{:S(2)}, u32[]{:S(2)}) collective-permute-start(f32[1,56,128]{2,1,0:T(8,128)S(1)} %get-tuple-element.26), channel_id=1, source_target_pairs={{0,4},{1,5},{2,6},{3,7},{4,0},{5,1},{6,2},{7,3},{8,12},{9,13},{10,... | collective-permute-start | bytes 86024 | tf_op jit(solution)/shard_map/ppermute | solution.py:499
  31.4 5.3 %collective-permute-start.8 = (f32[1,56,128]{2,1,0:T(8,128)S(1)}, f32[1,56,128]{2,1,0:T(8,128)S(1)}, u32[]{:S(2)}, u32[]{:S(2)}) collective-permute-start(f32[1,56,128]{2,1,0:T(8,128)S(1)} %get-tuple-element.25), channel_id=1, source_target_pairs={{0,13},{1,12},{2,15},{3,14},{4,9},{5,8},{6,11},{7,10},{8,5},{9,4},... | collective-permute-start | bytes 86024 | tf_op jit(solution)/shard_map/ppermute | solution.py:499

commit v2 on v1

--- a/solution.py
+++ b/solution.py
@@ -16,7 +16,8 @@
 I32 = jnp.int32
 PAD = 32
 LANES = 128
-CHUNKS = 3
+CHUNKS = 2
+LEAD = -1
 SPARE = 96
 
 
@@ -53,7 +54,7 @@
     return 0.1 + np.sin(np.pi * position) ** 2
 
 
-def front_kernel(half, aug_ref, w_in_hbm, w_plane_hbm, w_depth_hbm, w_head_hbm, x_hbm, plane_ref, depth_ref, head_ref, xs_ref, w_in_ref, w_plane_ref, w_depth_ref, w_head_ref, x_ref, big_ref, plane_scr, depth_scr, sems):
+def front_kernel(aug_ref, w_in_hbm, w_plane_hbm, w_depth_hbm, w_head_hbm, x_hbm, plane_ref, depth_ref, head_ref, xs_ref, w_in_ref, w_plane_ref, w_depth_ref, w_head_ref, x_ref, big_ref, plane_scr, depth_scr, sems):
     size = x_hbm.shape[2] // CHUNKS
     feats = [
         pltpu.make_async_copy(x_hbm.at[:, :, pl.ds(c * size, size)], x_ref.at[:, :, pl.ds(c * size, size)], sems.at[4 + c])
@@ -115,31 +116,14 @@
     head_ref[...] = jnp.where(at == (came ^ flip), wide, 0.0).astype(BF16)
 
     channels, depth, cells = x_ref.shape
-    rows = depth * PAD
-    margin = LANES
-    zeros = jnp.zeros((rows, margin), BF16)
-    for d in range(3):
-        xs_ref[d, :, pl.ds(0, margin)] = zeros
-        xs_ref[d, :, pl.ds(margin + cells, margin)] = zeros
-    size = cells // CHUNKS
-    column = iota((rows, size), 1)
-
-    def shift(c, d):
-        at = c * size
-        block = xs_ref[1, :, pl.ds(at, size + 2 * margin)]
-        moved = lax.slice_in_dim(block, margin + d - 1, margin + d - 1 + size, axis=1)
-        edge = (column + at) % half == (0 if d == 0 else half - 1)
-        xs_ref[d, :, pl.ds(margin + at, size)] = jnp.where(edge, jnp.zeros_like(moved), moved)
-
-    for c in range(CHUNKS):
+    zeros = jnp.zeros((depth * PAD, LANES), BF16)
+    xs_ref[:, pl.ds(0, LANES)] = zeros
+    xs_ref[:, pl.ds(LANES + cells, LANES)] = zeros
+    for c, copy in enumerate(feats):
         part = pl.ds(c * size, size)
-        feats[c].wait()
+        copy.wait()
         x = x_ref[:, :, part].reshape(channels * depth, size)
-        xs_ref[1, :, pl.ds(margin + c * size, size)] = jnp.dot(big_ref[...], x, preferred_element_type=F32).astype(BF16)
-        shift(c, 0)
-        if c > 0:
-            shift(c - 1, 2)
-    shift(CHUNKS - 1, 2)
+        xs_ref[:, pl.ds(LANES + c * size, size)] = jnp.dot(big_ref[...], x, preferred_element_type=F32).astype(BF16)
 
 
 def front(aug_code, w_in, w_plane, w_depth, w_head, feat):
@@ -149,10 +133,10 @@
     plane = (2, 4 * PAD, 6 * PAD)
     depth_w = (depth * PAD, depth * PAD)
     head = (4 * depth * maps, 4 * depth * PAD)
-    shifted = (3, depth * PAD, cells + 2 * LANES)
+    padded = (depth * PAD, cells + 2 * LANES)
     return pl.pallas_call(
-        functools.partial(front_kernel, math.isqrt(cells)),
-        out_shape=[jax.ShapeDtypeStruct(s, BF16) for s in (plane, depth_w, head, shifted)],
+        front_kernel,
+        out_shape=[jax.ShapeDtypeStruct(s, BF16) for s in (plane, depth_w, head, padded)],
         in_specs=[smem()] + [hbm()] * 5,
         out_specs=[vmem()] * 4,
         scratch_shapes=[
@@ -178,7 +162,7 @@
         anchor_out[...] = jnp.full(anchor_out.shape, anchor_ref[0], I32)
     else:
         out_ref, carry_out, a_ref = refs
-    _, rows, _ = xs_ref.shape
+    rows, _ = xs_ref.shape
     depth = rows // PAD
     step = 2 * LANES
     margin = LANES
@@ -188,10 +172,17 @@
         a_ref[pl.ds(0, carried)] = carry_in[...]
 
     def window_stage(t):
+        column = (iota((rows, step), 1) + t * step) % half
+        block = xs_ref[:, pl.ds(t * step, step + 2 * margin)]
         near = []
-        for d in range(3):
-            block = xs_ref[d, :, pl.ds(t * step, step + 2 * margin)]
-            near.append([lax.slice_in_dim(block, margin + half * e, margin + half * e + step, axis=1) for e in (-1, 0, 1)])
+        for d in (-1, 0, 1):
+            near.append([])
+            for e in (-1, 0, 1):
+                at = margin + half * e + d
+                one = lax.slice_in_dim(block, at, at + step, axis=1)
+                if d:
+                    one = jnp.where(column == (0 if d < 0 else half - 1), jnp.zeros_like(one), one)
+                near[-1].append(one)
         return near
 
     def plane_stage(near, z):
@@ -327,31 +318,28 @@
     return [(d, d ^ bit) for d in range(devices)]
 
 
-def slots_kernel(devices, bits, table_ref, anchor_ref, mine_ref, other_ref, window_ref, send_ref, keep_ref, place_ref):
+def slots_kernel(devices, bits, table_ref, anchor_ref, mine_ref, other_ref, window_ref, send_ref, keep_ref):
     me = lax.axis_index("patch")
     brick_rows = devices // 4
-
-    def note(b, _):
-        place_ref[table_ref[0, b]] = b
-        return 0
-
-    lax.fori_loop(0, devices, note, 0)
-    anchor = anchor_ref[0, 0]
+    brick = iota(table_ref.shape, 1)
+    row = lax.rem(brick // 4 - anchor_ref[:, :1] + brick_rows, jnp.full_like(brick, brick_rows))
+    place = row * 4 + brick % 4
+    owner = jnp.where(brick < devices, table_ref[...], -1)
     count = 1 << len(bits)
     _, rows, lanes = mine_ref.shape
     spare = iota((rows, lanes), 1) - jnp.where(iota((rows, lanes), 0) == rows - 8, SPARE, lanes)
+    places = []
     for s in range(count):
         mask = functools.reduce(lambda a, b: a ^ b, [bit for k, bit in enumerate(bits) if s >> (len(bits) - 1 - k) & 1], 0)
-        brick = place_ref[me ^ mask]
-        row = lax.rem(brick // 4 - anchor + brick_rows, brick_rows)
-        at = row * 4 + brick % 4
+        places.append(jnp.sum(jnp.where(owner == (me ^ mask), place, 0)))
+    for s, at in enumerate(places):
+        covered = at < 16
+        slot = at if brick_rows <= 4 else jnp.where(covered, at, 0)
+        value = (mine_ref[slot] + other_ref[slot]) * window_ref[slot]
+        value = jnp.where(spare == at // 4, 2.0, value)
+        value = jnp.where(spare == 4, 2.0 * (at % 4).astype(F32), value)
         if brick_rows > 4:
-            at = jnp.where(row < 4, at, 0)
-        value = (mine_ref[at] + other_ref[at]) * window_ref[at]
-        value = jnp.where(spare == row, 2.0, value)
-        value = jnp.where(spare == 4, 2.0 * (brick % 4).astype(F32), value)
-        if brick_rows > 4:
-            value = jnp.where(row < 4, value, 0.0)
+            value = jnp.where(covered, value, 0.0)
         if s < count // 2:
             keep_ref[s] = value
         else:
@@ -363,9 +351,8 @@
     return pl.pallas_call(
         functools.partial(slots_kernel, devices, bits),
         out_shape=[shape, shape],
-        in_specs=[smem()] * 2 + [vmem()] * 3,
+        in_specs=[vmem()] * 5,
         out_specs=[vmem()] * 2,
-        scratch_shapes=[pltpu.SMEM((devices,), I32)],
         compiler_params=params(),
         name="slots",
     )(table, anchor, mine, other, window)
@@ -468,20 +455,23 @@
     maps = w_head.shape[0]
     levels = [1 << k for k in range(devices.bit_length() - 1)]
     paired = levels[:1] + [bit | 1 for bit in levels[1:]]
-    bits = paired[1:-2] + [levels[-2], paired[-1]]
-
-    table = seed_table(brick_owner, devices)
-    tables = [table]
-    for bit in paired[1:] + paired[:1]:
-        got = lax.ppermute(tables[-1], "patch", partner(devices, bit))
-        tables.append(tables[-1] + got)
-    table = tables[-1]
+    bits = paired[1:-1] + [levels[-1]]
+
+    def table_round(k, table):
+        return table + lax.ppermute(table, "patch", partner(devices, rounds[k]))
+
+    rounds = paired[1:] + paired[:1]
+    table = table_round(0, seed_table(brick_owner, devices))
     plane, depth_w, head, shifted = front(aug_code, w_in, w_plane, w_depth, w_head, features[0])
     half = math.isqrt(cells)
     steps = cells // (2 * LANES)
-    ready = -(-half * half // 2 // (2 * LANES))
+    ready = -(-half * half // 2 // (2 * LANES)) + LEAD
     quarter = half * half // 4 // LANES
+    table = table_round(1, table)
     bricks, carry = patch_half(half, range(ready), (0,), quarter, False, aug_code, shifted, plane, depth_w, head)
+    patch_anchor, table = lax.optimization_barrier((patch_anchor, table))
+    for k in range(2, len(rounds)):
+        table = table_round(k, table)
     bricks, anchor = patch_half(
         half, range(ready, steps), (1, 2, 3), 0, True, aug_code, shifted, plane, depth_w, head, (carry, bricks, patch_anchor)
     )
@@ -495,8 +485,8 @@
         parts = [keep[c] + got[c] for c in cuts]
         if not last:
             keep, send = parts
-    far = [bits[-1], bits[-2], bits[-1] ^ bits[-2]]
-    others = [lax.ppermute(part, "patch", partner(devices, bit)) for part, bit in zip(parts[1:], far)]
+    far = [(3, bits[-1] ^ bits[-2]), (1, bits[-1]), (2, bits[-2])]
+    others = [lax.ppermute(parts[k], "patch", partner(devices, bit)) for k, bit in far]
     return finish(side, maps, depth, parts[0], others)
 
 

time: 37.8 us -> 36.1 us (0.955)
  Pallas kernels: 8.28 us -> 6.54 us
    pallas_call x2, Pallas kernels: 4.3 us -> 3.51 us  [patch_half(): pl.pallas_call(functools.partial(patch_kernel, half, tiles, brick_rows, k...]
    pallas_call x1, Pallas kernels: 0.79 us -> 0.27 us  [fill_slots(): pl.pallas_call(functools.partial(slots_kernel, devices, bits), out_shape=...]
    pallas_call x1, Pallas kernels: 2.3 us -> 1.87 us  [front(): pl.pallas_call(front_kernel, out_shape=[jax.ShapeDtypeStruct(s, BF16) for...]
  transfers between devices with their start and end apart: 9 -> 9, of which waited for: 8 -> 7; matrix products, arithmetic and copies ran while one was open for 0% -> 0% of each run, Pallas kernels for 0% -> 0%
where the time goes in v2:
time: 36.1 us; the launch traced here: 35.9 us
  waiting for transfers between devices  13.9 us (39%)
  starting transfers between devices  13.4 us (37%)
  Pallas kernels  6.54 us (18%)
  between operations  2.03 us (6%)
    ppermute x4, starting transfers between devices, table_round(): return table + lax.ppermute(table, 'patch', partner(devices, rounds[k]))  7.15 us
    ppermute x3, waiting for transfers between devices, on_device(): lax.ppermute(parts[k], 'patch', partner(devices, bit))  5.33 us
    ppermute x4, waiting for transfers between devices, table_round(): return table + lax.ppermute(table, 'patch', partner(devices, rounds[k]))  5.04 us
    ppermute x3, starting transfers between devices, on_device(): lax.ppermute(parts[k], 'patch', partner(devices, bit))  4.07 us
    ppermute x1, waiting for transfers between devices, on_device(): got = lax.ppermute(send, 'patch', partner(devices, bit))  3.56 us
    pallas_call x2, Pallas kernels, patch_half(): pl.pallas_call(functools.partial(patch_kernel, half, tiles, brick_rows, k...  3.51 us
    pallas_call x1, Pallas kernels, front(): pl.pallas_call(front_kernel, out_shape=[jax.ShapeDtypeStruct(s, BF16) for...  1.87 us
    ppermute x1, starting transfers between devices, on_device(): got = lax.ppermute(send, 'patch', partner(devices, bit))  1.6 us
  transfers between devices with their start and end apart: 9, of which 7 were waited for; matrix products, arithmetic and copies ran while one was open for 0% of the time, Pallas kernels for 0%

profile of v2, /device:TPU:0, one launch (start us, length us, event | category | flops | bytes accessed | tf_op | source)
XLA Modules:
  0.0 35.9 jit_solution(17180091367008955290)
XLA Ops:
  1.3 1.9 %front.1 = (bf16[2,128,192]{2,1,0:T(8,128)(2,1)S(1)}, bf16[128,128]{1,0:T(8,128)(2,1)S(1)}, bf16[48,512]{1,0:T(8,128)(2,1)S(1)}, bf16[128,2560]{1,0:T(8,128)(2,1)S(1)}) custom-call(s32[1]{0:T(128)S(6)} %copy.16.aug_ref, bf16[28,64]{1,0:T(8,128)(2,1)} %w_in_hbm.1, bf16[9,28,28]{2,1,0:T(8,128)(2,1)} %w_plane_hbm.1, bf16[3,28,28]{2,1,0:T(8,128)(2,1)} %w_depth_hbm.1, ...), custom_call_target="tpu_custom_call" | custom-call | flops 100000000 | bytes 1048576 | tf_op jit(solution)/shard_map/front/pallas_call | solution.py:137
  3.2 1.5 %shard_map.109 = (f32[16,56,128]{2,1,0:T(8,128)S(1)}, f32[4,48,128]{2,1,0:T(8,128)S(1)}) custom-call(s32[1]{0:T(128)S(6)} %copy.16.aug_ref, bf16[128,2560]{1,0:T(8,128)(2,1)S(1)} %get-tuple-element.18.xs_ref, bf16[2,128,192]{2,1,0:T(8,128)(2,1)S(1)} %get-tuple-element.19.plane_ref, bf16[128,128]{1,0:T(8,128)(2,1)S(1)} %get-tuple-element.20.depth_ref, ...), custom_call_target="tpu_custom_call" | custom-call | flops 1000000000 | bytes 1048576 | tf_op jit(solution)/shard_map/pallas_call | solution.py:288
  4.7 0.0 copy-start
  4.7 2.0 %shard_map.110 = (f32[16,56,128]{2,1,0:T(8,128)S(1)}, s32[1,128]{1,0:T(1,128)S(1)}) custom-call(s32[1]{0:T(128)S(6)} %copy.16.aug_ref, bf16[128,2560]{1,0:T(8,128)(2,1)S(1)} %get-tuple-element.18.xs_ref, bf16[2,128,192]{2,1,0:T(8,128)(2,1)S(1)} %get-tuple-element.19.plane_ref, ...), custom_call_target="tpu_custom_call", output_to_operand_aliasing={{0}: (6, {})} | custom-call | flops 1000000000 | bytes 1048576 | tf_op jit(solution)/shard_map/pallas_call | solution.py:288
  6.7 0.0 copy-start.1
  6.7 0.0 copy-start.2
  6.7 0.6 %collective-permute-start.4 = (f32[16,56,128]{2,1,0:T(8,128)S(1)}, f32[16,56,128]{2,1,0:T(8,128)S(1)}, u32[]{:S(2)}, u32[]{:S(2)}) collective-permute-start(f32[16,56,128]{2,1,0:T(8,128)S(1)} %get-tuple-element.26.mine_ref), channel_id=1, source_target_pairs={{0,1},{1,0},{2,3},{3,2},{4,5},{5,4},{6,7},{7,6},{8,9},{9,8},{10,11... | collective-permute-start | bytes 1376264 | tf_op jit(solution)/shard_map/ppermute | solution.py:478
  8.0 2.7 %collective-permute-start = (s32[1,128]{1,0:T(1,128)S(1)}, s32[1,128]{1,0:T(1,128)S(1)}, u32[]{:S(2)}, u32[]{:S(2)}) collective-permute-start(s32[1,128]{1,0:T(1,128)S(1)} %seed.1), channel_id=1, source_target_pairs={{0,3},{1,2},{2,1},{3,0},{4,7},{5,6},{6,5},{7,4},{8,11},{9,10},{10,... | collective-permute-start | bytes 1544 | tf_op jit(solution)/shard_map/ppermute | solution.py:461
  10.7 1.3 %collective-permute-done = s32[1,128]{1,0:T(1,128)S(1)} collective-permute-done((s32[1,128]{1,0:T(1,128)S(1)}, s32[1,128]{1,0:T(1,128)S(1)}, u32[]{:S(2)}, u32[]{:S(2)}) %collective-permute-start) | collective-permute-done | bytes 544 | tf_op jit(solution)/shard_map/ppermute | solution.py:461
  12.0 1.7 %collective-permute-start.1 = (s32[1,128]{1,0:T(1,128)S(1)}, s32[1,128]{1,0:T(1,128)S(1)}, u32[]{:S(2)}, u32[]{:S(2)}) collective-permute-start(s32[1,128]{1,0:T(1,128)S(1)} %add.24), channel_id=1, source_target_pairs={{0,5},{1,4},{2,7},{3,6},{4,1},{5,0},{6,3},{7,2},{8,13},{9,12},{10,... | collective-permute-start | bytes 1544 | tf_op jit(solution)/shard_map/ppermute | solution.py:461
  13.7 1.3 %collective-permute-done.1 = s32[1,128]{1,0:T(1,128)S(1)} collective-permute-done((s32[1,128]{1,0:T(1,128)S(1)}, s32[1,128]{1,0:T(1,128)S(1)}, u32[]{:S(2)}, u32[]{:S(2)}) %collective-permute-start.1) | collective-permute-done | bytes 544 | tf_op jit(solution)/shard_map/ppermute | solution.py:461
  15.0 2.7 %collective-permute-start.2 = (s32[1,128]{1,0:T(1,128)S(1)}, s32[1,128]{1,0:T(1,128)S(1)}, u32[]{:S(2)}, u32[]{:S(2)}) collective-permute-start(s32[1,128]{1,0:T(1,128)S(1)} %add.25), channel_id=1, source_target_pairs={{0,9},{1,8},{2,11},{3,10},{4,13},{5,12},{6,15},{7,14},{8,1},{9,0},... | collective-permute-start | bytes 1544 | tf_op jit(solution)/shard_map/ppermute | solution.py:461
  17.7 1.3 %collective-permute-done.2 = s32[1,128]{1,0:T(1,128)S(1)} collective-permute-done((s32[1,128]{1,0:T(1,128)S(1)}, s32[1,128]{1,0:T(1,128)S(1)}, u32[]{:S(2)}, u32[]{:S(2)}) %collective-permute-start.2) | collective-permute-done | bytes 544 | tf_op jit(solution)/shard_map/ppermute | solution.py:461
  19.0 0.0 collective-permute-start.3
  19.0 1.2 %collective-permute-done.3 = s32[1,128]{1,0:T(1,128)S(1)} collective-permute-done((s32[1,128]{1,0:T(1,128)S(1)}, s32[1,128]{1,0:T(1,128)S(1)}, u32[]{:S(2)}, u32[]{:S(2)}) %collective-permute-start.3) | collective-permute-done | bytes 544 | tf_op jit(solution)/shard_map/ppermute | solution.py:461
  20.2 0.0 collective-permute-done.4.other_ref
  20.2 0.0 copy-done
  20.2 0.3 slots.1
  20.5 1.6 %collective-permute-start.5 = (f32[4,56,128]{2,1,0:T(8,128)S(1)}, f32[4,56,128]{2,1,0:T(8,128)S(1)}, u32[]{:S(2)}, u32[]{:S(2)}) collective-permute-start(f32[4,56,128]{2,1,0:T(8,128)S(1)} %get-tuple-element.28), channel_id=1, source_target_pairs={{0,3},{1,2},{2,1},{3,0},{4,7},{5,6},{6,5},{7,4},{8,11},{9,10},{10,... | collective-permute-start | bytes 344072 | tf_op jit(solution)/shard_map/ppermute | solution.py:481
  22.1 3.6 %collective-permute-done.5 = f32[4,56,128]{2,1,0:T(8,128)S(1)} collective-permute-done((f32[4,56,128]{2,1,0:T(8,128)S(1)}, f32[4,56,128]{2,1,0:T(8,128)S(1)}, u32[]{:S(2)}, u32[]{:S(2)}) %collective-permute-start.5) | collective-permute-done | bytes 114720 | tf_op jit(solution)/shard_map/ppermute | solution.py:481
  25.6 1.5 %collective-permute-start.8 = (f32[1,56,128]{2,1,0:T(8,128)S(1)}, f32[1,56,128]{2,1,0:T(8,128)S(1)}, u32[]{:S(2)}, u32[]{:S(2)}) collective-permute-start(f32[1,56,128]{2,1,0:T(8,128)S(1)} %get-tuple-element.29), channel_id=1, source_target_pairs={{0,5},{1,4},{2,7},{3,6},{4,1},{5,0},{6,3},{7,2},{8,13},{9,12},{10,... | collective-permute-start | bytes 86024 | tf_op jit(solution)/shard_map/ppermute | solution.py:489
  27.1 2.6 %collective-permute-start.7 = (f32[1,56,128]{2,1,0:T(8,128)S(1)}, f32[1,56,128]{2,1,0:T(8,128)S(1)}, u32[]{:S(2)}, u32[]{:S(2)}) collective-permute-start(f32[1,56,128]{2,1,0:T(8,128)S(1)} %get-tuple-element.30), channel_id=1, source_target_pairs={{0,8},{1,9},{2,10},{3,11},{4,12},{5,13},{6,14},{7,15},{8,0},{9,1},... | collective-permute-start | bytes 86024 | tf_op jit(solution)/shard_map/ppermute | solution.py:489
  29.7 0.0 collective-permute-start.6
  29.7 0.0 collective-permute-done.8.c_ref
  29.7 2.4 %collective-permute-done.7.b_ref = f32[1,56,128]{2,1,0:T(8,128)S(1)} collective-permute-done((f32[1,56,128]{2,1,0:T(8,128)S(1)}, f32[1,56,128]{2,1,0:T(8,128)S(1)}, u32[]{:S(2)}, u32[]{:S(2)}) %collective-permute-start.7) | collective-permute-done | bytes 28704 | tf_op jit(solution)/shard_map/ppermute | solution.py:489
  32.2 2.9 %collective-permute-done.6.a_ref = f32[1,56,128]{2,1,0:T(8,128)S(1)} collective-permute-done((f32[1,56,128]{2,1,0:T(8,128)S(1)}, f32[1,56,128]{2,1,0:T(8,128)S(1)}, u32[]{:S(2)}, u32[]{:S(2)}) %collective-permute-start.6) | collective-permute-done | bytes 28704 | tf_op jit(solution)/shard_map/ppermute | solution.py:489
  35.1 0.0 copy-done.1
  35.1 0.0 copy-done.2
  35.1 0.9 %brick.1 = f32[1,4,2304]{2,1,0:T(4,128)} custom-call(f32[1,56,128]{2,1,0:T(8,128)S(1)} %get-tuple-element.32.mine_ref, f32[1,56,128]{2,1,0:T(8,128)S(1)} %collective-permute-done.6.a_ref, f32[1,56,128]{2,1,0:T(8,128)S(1)} %collective-permute-done.7.b_ref, f32[1,56,128]{2,1,0:T(8,128)S(1)} %collective-permute-done.8.c_ref, f32[4,640]{1,0:T(4,128)S(1)} %copy-done.2, ...), custom_call_target="tpu_custom_call" | custom-call | tf_op jit(solution)/shard_map/brick/pallas_call | solution.py:421
  (6 shorter events, 0.0 us)
Async XLA Ops:
  4.7 15.5 %copy-start = (f32[16,56,128]{2,1,0:T(8,128)S(1)}, f32[16,56,128]{2,1,0:T(8,128)}, u32[]{:S(2)}) copy-start(f32[16,56,128]{2,1,0:T(8,128)} %constant.6.clone.window_ref) | copy-start | bytes 1376260
  6.7 28.3 %copy-start.1 = (f32[4,640]{1,0:T(4,128)S(1)}, f32[4,640]{1,0:T(4,128)}, u32[]{:S(2)}) copy-start(f32[4,640]{1,0:T(4,128)} %constant.8.clone.cols_ref) | copy-start | bytes 30724
  6.7 28.3 %copy-start.2 = (f32[4,640]{1,0:T(4,128)S(1)}, f32[4,640]{1,0:T(4,128)}, u32[]{:S(2)}) copy-start(f32[4,640]{1,0:T(4,128)} %constant.7.clone.rows_ref) | copy-start | bytes 30724
  6.7 13.4 %collective-permute-start.4 = (f32[16,56,128]{2,1,0:T(8,128)S(1)}, f32[16,56,128]{2,1,0:T(8,128)S(1)}, u32[]{:S(2)}, u32[]{:S(2)}) collective-permute-start(f32[16,56,128]{2,1,0:T(8,128)S(1)} %get-tuple-element.26.mine_ref), channel_id=1, source_target_pairs={{0,1},{1,0},{2,3},{3,2},{4,5},{5,4},{6,7},{7,6},{8,9},{9,8},{10,11... | collective-permute-start | bytes 1376264 | tf_op jit(solution)/shard_map/ppermute | solution.py:478
  8.0 4.0 %collective-permute-start = (s32[1,128]{1,0:T(1,128)S(1)}, s32[1,128]{1,0:T(1,128)S(1)}, u32[]{:S(2)}, u32[]{:S(2)}) collective-permute-start(s32[1,128]{1,0:T(1,128)S(1)} %seed.1), channel_id=1, source_target_pairs={{0,3},{1,2},{2,1},{3,0},{4,7},{5,6},{6,5},{7,4},{8,11},{9,10},{10,... | collective-permute-start | bytes 1544 | tf_op jit(solution)/shard_map/ppermute | solution.py:461
  12.0 3.0 %collective-permute-start.1 = (s32[1,128]{1,0:T(1,128)S(1)}, s32[1,128]{1,0:T(1,128)S(1)}, u32[]{:S(2)}, u32[]{:S(2)}) collective-permute-start(s32[1,128]{1,0:T(1,128)S(1)} %add.24), channel_id=1, source_target_pairs={{0,5},{1,4},{2,7},{3,6},{4,1},{5,0},{6,3},{7,2},{8,13},{9,12},{10,... | collective-permute-start | bytes 1544 | tf_op jit(solution)/shard_map/ppermute | solution.py:461
  15.0 4.0 %collective-permute-start.2 = (s32[1,128]{1,0:T(1,128)S(1)}, s32[1,128]{1,0:T(1,128)S(1)}, u32[]{:S(2)}, u32[]{:S(2)}) collective-permute-start(s32[1,128]{1,0:T(1,128)S(1)} %add.25), channel_id=1, source_target_pairs={{0,9},{1,8},{2,11},{3,10},{4,13},{5,12},{6,15},{7,14},{8,1},{9,0},... | collective-permute-start | bytes 1544 | tf_op jit(solution)/shard_map/ppermute | solution.py:461
  19.0 1.2 %collective-permute-start.3 = (s32[1,128]{1,0:T(1,128)S(1)}, s32[1,128]{1,0:T(1,128)S(1)}, u32[]{:S(2)}, u32[]{:S(2)}) collective-permute-start(s32[1,128]{1,0:T(1,128)S(1)} %add.26), channel_id=1, source_target_pairs={{0,1},{1,0},{2,3},{3,2},{4,5},{5,4},{6,7},{7,6},{8,9},{9,8},{10,11... | collective-permute-start | bytes 1544 | tf_op jit(solution)/shard_map/ppermute | solution.py:461
  20.5 5.2 %collective-permute-start.5 = (f32[4,56,128]{2,1,0:T(8,128)S(1)}, f32[4,56,128]{2,1,0:T(8,128)S(1)}, u32[]{:S(2)}, u32[]{:S(2)}) collective-permute-start(f32[4,56,128]{2,1,0:T(8,128)S(1)} %get-tuple-element.28), channel_id=1, source_target_pairs={{0,3},{1,2},{2,1},{3,0},{4,7},{5,6},{6,5},{7,4},{8,11},{9,10},{10,... | collective-permute-start | bytes 344072 | tf_op jit(solution)/shard_map/ppermute | solution.py:481
  25.6 4.1 %collective-permute-start.8 = (f32[1,56,128]{2,1,0:T(8,128)S(1)}, f32[1,56,128]{2,1,0:T(8,128)S(1)}, u32[]{:S(2)}, u32[]{:S(2)}) collective-permute-start(f32[1,56,128]{2,1,0:T(8,128)S(1)} %get-tuple-element.29), channel_id=1, source_target_pairs={{0,5},{1,4},{2,7},{3,6},{4,1},{5,0},{6,3},{7,2},{8,13},{9,12},{10,... | collective-permute-start | bytes 86024 | tf_op jit(solution)/shard_map/ppermute | solution.py:489
  27.1 5.0 %collective-permute-start.7 = (f32[1,56,128]{2,1,0:T(8,128)S(1)}, f32[1,56,128]{2,1,0:T(8,128)S(1)}, u32[]{:S(2)}, u32[]{:S(2)}) collective-permute-start(f32[1,56,128]{2,1,0:T(8,128)S(1)} %get-tuple-element.30), channel_id=1, source_target_pairs={{0,8},{1,9},{2,10},{3,11},{4,12},{5,13},{6,14},{7,15},{8,0},{9,1},... | collective-permute-start | bytes 86024 | tf_op jit(solution)/shard_map/ppermute | solution.py:489
  29.7 5.3 %collective-permute-start.6 = (f32[1,56,128]{2,1,0:T(8,128)S(1)}, f32[1,56,128]{2,1,0:T(8,128)S(1)}, u32[]{:S(2)}, u32[]{:S(2)}) collective-permute-start(f32[1,56,128]{2,1,0:T(8,128)S(1)} %get-tuple-element.31), channel_id=1, source_target_pairs={{0,13},{1,12},{2,15},{3,14},{4,9},{5,8},{6,11},{7,10},{8,5},{9,4},... | collective-permute-start | bytes 86024 | tf_op jit(solution)/shard_map/ppermute | solution.py:489

commit v3 on v2

--- a/solution.py
+++ b/solution.py
@@ -17,7 +17,7 @@
 PAD = 32
 LANES = 128
 CHUNKS = 2
-LEAD = -1
+LEAD = 1
 SPARE = 96
 
 
@@ -460,20 +460,21 @@
     def table_round(k, table):
         return table + lax.ppermute(table, "patch", partner(devices, rounds[k]))
 
-    rounds = paired[1:] + paired[:1]
-    table = table_round(0, seed_table(brick_owner, devices))
+    rounds = paired
+    table = seed_table(brick_owner, devices)
+    for k in range(len(rounds)):
+        table = table_round(k, table)
     plane, depth_w, head, shifted = front(aug_code, w_in, w_plane, w_depth, w_head, features[0])
     half = math.isqrt(cells)
     steps = cells // (2 * LANES)
     ready = -(-half * half // 2 // (2 * LANES)) + LEAD
-    quarter = half * half // 4 // LANES
-    table = table_round(1, table)
-    bricks, carry = patch_half(half, range(ready), (0,), quarter, False, aug_code, shifted, plane, depth_w, head)
-    patch_anchor, table = lax.optimization_barrier((patch_anchor, table))
-    for k in range(2, len(rounds)):
-        table = table_round(k, table)
+    starts = [half * half * i // 4 // LANES for i in range(4)]
+    span = -(-half * half // 4 // LANES)
+    early = [i for i in range(4) if starts[i] + span < 2 * ready]
+    late = [i for i in range(4) if i not in early]
+    bricks, carry = patch_half(half, range(ready), early, starts[late[0]], False, aug_code, shifted, plane, depth_w, head)
     bricks, anchor = patch_half(
-        half, range(ready, steps), (1, 2, 3), 0, True, aug_code, shifted, plane, depth_w, head, (carry, bricks, patch_anchor)
+        half, range(ready, steps), late, 0, True, aug_code, shifted, plane, depth_w, head, (carry, bricks, patch_anchor)
     )
     other = lax.ppermute(bricks, "patch", partner(devices, 1))
     send, keep = fill_slots(devices, bits, table, anchor, bricks, other, wire_window(side, maps, depth))

time: 36.1 us -> 35.1 us (0.972)
  waiting for transfers between devices: 13.9 us -> 13 us
    ppermute x3, waiting for transfers between devices: 5.33 us -> 4.34 us  [on_device(): lax.ppermute(parts[k], 'patch', partner(devices, bit))]
where the time goes in v3:
time: 35.1 us; the launch traced here: 35 us
  starting transfers between devices  13.2 us (38%)
  waiting for transfers between devices  13 us (37%)
  Pallas kernels  6.7 us (19%)
  between operations  2.03 us (6%)
    ppermute x4, starting transfers between devices, table_round(): return table + lax.ppermute(table, 'patch', partner(devices, rounds[k]))  7.17 us
    ppermute x4, waiting for transfers between devices, table_round(): return table + lax.ppermute(table, 'patch', partner(devices, rounds[k]))  5.03 us
    ppermute x3, waiting for transfers between devices, on_device(): lax.ppermute(parts[k], 'patch', partner(devices, bit))  4.34 us
    ppermute x3, starting transfers between devices, on_device(): lax.ppermute(parts[k], 'patch', partner(devices, bit))  3.89 us
    pallas_call x2, Pallas kernels, patch_half(): pl.pallas_call(functools.partial(patch_kernel, half, tiles, brick_rows, k...  3.66 us
    ppermute x1, waiting for transfers between devices, on_device(): got = lax.ppermute(send, 'patch', partner(devices, bit))  3.61 us
    pallas_call x1, Pallas kernels, front(): pl.pallas_call(front_kernel, out_shape=[jax.ShapeDtypeStruct(s, BF16) for...  1.87 us
    ppermute x1, starting transfers between devices, on_device(): got = lax.ppermute(send, 'patch', partner(devices, bit))  1.6 us
  transfers between devices with their start and end apart: 9, of which 7 were waited for; matrix products, arithmetic and copies ran while one was open for 0% of the time, Pallas kernels for 0%

profile of v3, /device:TPU:0, one launch (start us, length us, event | category | flops | bytes accessed | tf_op | source)
XLA Modules:
  0.0 35.0 jit_solution(3023089964775412322)
XLA Ops:
  1.3 1.9 %front.1 = (bf16[2,128,192]{2,1,0:T(8,128)(2,1)S(1)}, bf16[128,128]{1,0:T(8,128)(2,1)S(1)}, bf16[48,512]{1,0:T(8,128)(2,1)S(1)}, bf16[128,2560]{1,0:T(8,128)(2,1)S(1)}) custom-call(s32[1]{0:T(128)S(6)} %copy.16.aug_ref, bf16[28,64]{1,0:T(8,128)(2,1)} %w_in_hbm.1, bf16[9,28,28]{2,1,0:T(8,128)(2,1)} %w_plane_hbm.1, bf16[3,28,28]{2,1,0:T(8,128)(2,1)} %w_depth_hbm.1, ...), custom_call_target="tpu_custom_call" | custom-call | flops 100000000 | bytes 1048576 | tf_op jit(solution)/shard_map/front/pallas_call | solution.py:137
  3.2 2.2 %shard_map.109 = (f32[16,56,128]{2,1,0:T(8,128)S(1)}, f32[3,48,128]{2,1,0:T(8,128)S(1)}) custom-call(s32[1]{0:T(128)S(6)} %copy.16.aug_ref, bf16[128,2560]{1,0:T(8,128)(2,1)S(1)} %get-tuple-element.15.xs_ref, bf16[2,128,192]{2,1,0:T(8,128)(2,1)S(1)} %get-tuple-element.16.plane_ref, bf16[128,128]{1,0:T(8,128)(2,1)S(1)} %get-tuple-element.17.depth_ref, ...), custom_call_target="tpu_custom_call" | custom-call | flops 1000000000 | bytes 1048576 | tf_op jit(solution)/shard_map/pallas_call | solution.py:288
  5.4 0.0 copy-start
  5.4 1.4 %shard_map.110 = (f32[16,56,128]{2,1,0:T(8,128)S(1)}, s32[1,128]{1,0:T(1,128)S(1)}) custom-call(s32[1]{0:T(128)S(6)} %copy.16.aug_ref, bf16[128,2560]{1,0:T(8,128)(2,1)S(1)} %get-tuple-element.15.xs_ref, bf16[2,128,192]{2,1,0:T(8,128)(2,1)S(1)} %get-tuple-element.16.plane_ref, ...), custom_call_target="tpu_custom_call", output_to_operand_aliasing={{0}: (6, {})} | custom-call | flops 1000000000 | bytes 1048576 | tf_op jit(solution)/shard_map/pallas_call | solution.py:288
  6.9 0.0 copy-start.1
  6.9 0.0 copy-start.2
  6.9 0.6 %collective-permute-start.4 = (f32[16,56,128]{2,1,0:T(8,128)S(1)}, f32[16,56,128]{2,1,0:T(8,128)S(1)}, u32[]{:S(2)}, u32[]{:S(2)}) collective-permute-start(f32[16,56,128]{2,1,0:T(8,128)S(1)} %get-tuple-element.22.mine_ref), channel_id=1, source_target_pairs={{0,1},{1,0},{2,3},{3,2},{4,5},{5,4},{6,7},{7,6},{8,9},{9,8},{10,11... | collective-permute-start | bytes 1376264 | tf_op jit(solution)/shard_map/ppermute | solution.py:479
  8.1 0.1 collective-permute-start
  8.2 1.1 %collective-permute-done = s32[1,128]{1,0:T(1,128)S(1)} collective-permute-done((s32[1,128]{1,0:T(1,128)S(1)}, s32[1,128]{1,0:T(1,128)S(1)}, u32[]{:S(2)}, u32[]{:S(2)}) %collective-permute-start) | collective-permute-done | bytes 544 | tf_op jit(solution)/shard_map/ppermute | solution.py:461
  9.3 2.6 %collective-permute-start.1 = (s32[1,128]{1,0:T(1,128)S(1)}, s32[1,128]{1,0:T(1,128)S(1)}, u32[]{:S(2)}, u32[]{:S(2)}) collective-permute-start(s32[1,128]{1,0:T(1,128)S(1)} %add.24), channel_id=1, source_target_pairs={{0,3},{1,2},{2,1},{3,0},{4,7},{5,6},{6,5},{7,4},{8,11},{9,10},{10,... | collective-permute-start | bytes 1544 | tf_op jit(solution)/shard_map/ppermute | solution.py:461
  12.0 1.3 %collective-permute-done.1 = s32[1,128]{1,0:T(1,128)S(1)} collective-permute-done((s32[1,128]{1,0:T(1,128)S(1)}, s32[1,128]{1,0:T(1,128)S(1)}, u32[]{:S(2)}, u32[]{:S(2)}) %collective-permute-start.1) | collective-permute-done | bytes 544 | tf_op jit(solution)/shard_map/ppermute | solution.py:461
  13.3 1.8 %collective-permute-start.2 = (s32[1,128]{1,0:T(1,128)S(1)}, s32[1,128]{1,0:T(1,128)S(1)}, u32[]{:S(2)}, u32[]{:S(2)}) collective-permute-start(s32[1,128]{1,0:T(1,128)S(1)} %add.25), channel_id=1, source_target_pairs={{0,5},{1,4},{2,7},{3,6},{4,1},{5,0},{6,3},{7,2},{8,13},{9,12},{10,... | collective-permute-start | bytes 1544 | tf_op jit(solution)/shard_map/ppermute | solution.py:461
  15.0 1.3 %collective-permute-done.2 = s32[1,128]{1,0:T(1,128)S(1)} collective-permute-done((s32[1,128]{1,0:T(1,128)S(1)}, s32[1,128]{1,0:T(1,128)S(1)}, u32[]{:S(2)}, u32[]{:S(2)}) %collective-permute-start.2) | collective-permute-done | bytes 544 | tf_op jit(solution)/shard_map/ppermute | solution.py:461
  16.3 2.7 %collective-permute-start.3 = (s32[1,128]{1,0:T(1,128)S(1)}, s32[1,128]{1,0:T(1,128)S(1)}, u32[]{:S(2)}, u32[]{:S(2)}) collective-permute-start(s32[1,128]{1,0:T(1,128)S(1)} %add.26), channel_id=1, source_target_pairs={{0,9},{1,8},{2,11},{3,10},{4,13},{5,12},{6,15},{7,14},{8,1},{9,0},... | collective-permute-start | bytes 1544 | tf_op jit(solution)/shard_map/ppermute | solution.py:461
  19.0 1.3 %collective-permute-done.3 = s32[1,128]{1,0:T(1,128)S(1)} collective-permute-done((s32[1,128]{1,0:T(1,128)S(1)}, s32[1,128]{1,0:T(1,128)S(1)}, u32[]{:S(2)}, u32[]{:S(2)}) %collective-permute-start.3) | collective-permute-done | bytes 544 | tf_op jit(solution)/shard_map/ppermute | solution.py:461
  20.3 0.0 collective-permute-done.4.other_ref
  20.3 0.0 copy-done
  20.3 0.3 slots.1
  20.6 1.6 %collective-permute-start.5 = (f32[4,56,128]{2,1,0:T(8,128)S(1)}, f32[4,56,128]{2,1,0:T(8,128)S(1)}, u32[]{:S(2)}, u32[]{:S(2)}) collective-permute-start(f32[4,56,128]{2,1,0:T(8,128)S(1)} %get-tuple-element.24), channel_id=1, source_target_pairs={{0,3},{1,2},{2,1},{3,0},{4,7},{5,6},{6,5},{7,4},{8,11},{9,10},{10,... | collective-permute-start | bytes 344072 | tf_op jit(solution)/shard_map/ppermute | solution.py:482
  22.2 3.6 %collective-permute-done.5 = f32[4,56,128]{2,1,0:T(8,128)S(1)} collective-permute-done((f32[4,56,128]{2,1,0:T(8,128)S(1)}, f32[4,56,128]{2,1,0:T(8,128)S(1)}, u32[]{:S(2)}, u32[]{:S(2)}) %collective-permute-start.5) | collective-permute-done | bytes 114720 | tf_op jit(solution)/shard_map/ppermute | solution.py:482
  25.8 3.5 %collective-permute-start.6 = (f32[1,56,128]{2,1,0:T(8,128)S(1)}, f32[1,56,128]{2,1,0:T(8,128)S(1)}, u32[]{:S(2)}, u32[]{:S(2)}) collective-permute-start(f32[1,56,128]{2,1,0:T(8,128)S(1)} %get-tuple-element.27), channel_id=1, source_target_pairs={{0,13},{1,12},{2,15},{3,14},{4,9},{5,8},{6,11},{7,10},{8,5},{9,4},... | collective-permute-start | bytes 86024 | tf_op jit(solution)/shard_map/ppermute | solution.py:490
  29.3 0.0 collective-permute-start.7
  29.3 0.4 %collective-permute-start.8 = (f32[1,56,128]{2,1,0:T(8,128)S(1)}, f32[1,56,128]{2,1,0:T(8,128)S(1)}, u32[]{:S(2)}, u32[]{:S(2)}) collective-permute-start(f32[1,56,128]{2,1,0:T(8,128)S(1)} %get-tuple-element.25), channel_id=1, source_target_pairs={{0,5},{1,4},{2,7},{3,6},{4,1},{5,0},{6,3},{7,2},{8,13},{9,12},{10,... | collective-permute-start | bytes 86024 | tf_op jit(solution)/shard_map/ppermute | solution.py:490
  29.7 1.3 %collective-permute-done.6.a_ref = f32[1,56,128]{2,1,0:T(8,128)S(1)} collective-permute-done((f32[1,56,128]{2,1,0:T(8,128)S(1)}, f32[1,56,128]{2,1,0:T(8,128)S(1)}, u32[]{:S(2)}, u32[]{:S(2)}) %collective-permute-start.6) | collective-permute-done | bytes 28704 | tf_op jit(solution)/shard_map/ppermute | solution.py:490
  31.0 3.1 %collective-permute-done.7.b_ref = f32[1,56,128]{2,1,0:T(8,128)S(1)} collective-permute-done((f32[1,56,128]{2,1,0:T(8,128)S(1)}, f32[1,56,128]{2,1,0:T(8,128)S(1)}, u32[]{:S(2)}, u32[]{:S(2)}) %collective-permute-start.7) | collective-permute-done | bytes 28704 | tf_op jit(solution)/shard_map/ppermute | solution.py:490
  34.1 0.0 collective-permute-done.8.c_ref
  34.1 0.0 copy-done.1
  34.1 0.0 copy-done.2
  34.1 0.9 %brick.1 = f32[1,4,2304]{2,1,0:T(4,128)} custom-call(f32[1,56,128]{2,1,0:T(8,128)S(1)} %get-tuple-element.28.mine_ref, f32[1,56,128]{2,1,0:T(8,128)S(1)} %collective-permute-done.6.a_ref, f32[1,56,128]{2,1,0:T(8,128)S(1)} %collective-permute-done.7.b_ref, f32[1,56,128]{2,1,0:T(8,128)S(1)} %collective-permute-done.8.c_ref, f32[4,640]{1,0:T(4,128)S(1)} %copy-done.1, ...), custom_call_target="tpu_custom_call" | custom-call | tf_op jit(solution)/shard_map/brick/pallas_call | solution.py:421
  (6 shorter events, 0.0 us)
Async XLA Ops:
  5.4 14.9 %copy-start = (f32[16,56,128]{2,1,0:T(8,128)S(1)}, f32[16,56,128]{2,1,0:T(8,128)}, u32[]{:S(2)}) copy-start(f32[16,56,128]{2,1,0:T(8,128)} %constant.6.clone.window_ref) | copy-start | bytes 1376260
  6.9 27.2 %copy-start.1 = (f32[4,640]{1,0:T(4,128)S(1)}, f32[4,640]{1,0:T(4,128)}, u32[]{:S(2)}) copy-start(f32[4,640]{1,0:T(4,128)} %constant.7.clone.rows_ref) | copy-start | bytes 30724
  6.9 27.2 %copy-start.2 = (f32[4,640]{1,0:T(4,128)S(1)}, f32[4,640]{1,0:T(4,128)}, u32[]{:S(2)}) copy-start(f32[4,640]{1,0:T(4,128)} %constant.8.clone.cols_ref) | copy-start | bytes 30724
  6.9 13.4 %collective-permute-start.4 = (f32[16,56,128]{2,1,0:T(8,128)S(1)}, f32[16,56,128]{2,1,0:T(8,128)S(1)}, u32[]{:S(2)}, u32[]{:S(2)}) collective-permute-start(f32[16,56,128]{2,1,0:T(8,128)S(1)} %get-tuple-element.22.mine_ref), channel_id=1, source_target_pairs={{0,1},{1,0},{2,3},{3,2},{4,5},{5,4},{6,7},{7,6},{8,9},{9,8},{10,11... | collective-permute-start | bytes 1376264 | tf_op jit(solution)/shard_map/ppermute | solution.py:479
  8.1 1.2 %collective-permute-start = (s32[1,128]{1,0:T(1,128)S(1)}, s32[1,128]{1,0:T(1,128)S(1)}, u32[]{:S(2)}, u32[]{:S(2)}) collective-permute-start(s32[1,128]{1,0:T(1,128)S(1)} %seed.1), channel_id=1, source_target_pairs={{0,1},{1,0},{2,3},{3,2},{4,5},{5,4},{6,7},{7,6},{8,9},{9,8},{10,11... | collective-permute-start | bytes 1544 | tf_op jit(solution)/shard_map/ppermute | solution.py:461
  9.3 3.9 %collective-permute-start.1 = (s32[1,128]{1,0:T(1,128)S(1)}, s32[1,128]{1,0:T(1,128)S(1)}, u32[]{:S(2)}, u32[]{:S(2)}) collective-permute-start(s32[1,128]{1,0:T(1,128)S(1)} %add.24), channel_id=1, source_target_pairs={{0,3},{1,2},{2,1},{3,0},{4,7},{5,6},{6,5},{7,4},{8,11},{9,10},{10,... | collective-permute-start | bytes 1544 | tf_op jit(solution)/shard_map/ppermute | solution.py:461
  13.3 3.1 %collective-permute-start.2 = (s32[1,128]{1,0:T(1,128)S(1)}, s32[1,128]{1,0:T(1,128)S(1)}, u32[]{:S(2)}, u32[]{:S(2)}) collective-permute-start(s32[1,128]{1,0:T(1,128)S(1)} %add.25), channel_id=1, source_target_pairs={{0,5},{1,4},{2,7},{3,6},{4,1},{5,0},{6,3},{7,2},{8,13},{9,12},{10,... | collective-permute-start | bytes 1544 | tf_op jit(solution)/shard_map/ppermute | solution.py:461
  16.3 4.0 %collective-permute-start.3 = (s32[1,128]{1,0:T(1,128)S(1)}, s32[1,128]{1,0:T(1,128)S(1)}, u32[]{:S(2)}, u32[]{:S(2)}) collective-permute-start(s32[1,128]{1,0:T(1,128)S(1)} %add.26), channel_id=1, source_target_pairs={{0,9},{1,8},{2,11},{3,10},{4,13},{5,12},{6,15},{7,14},{8,1},{9,0},... | collective-permute-start | bytes 1544 | tf_op jit(solution)/shard_map/ppermute | solution.py:461
  20.6 5.2 %collective-permute-start.5 = (f32[4,56,128]{2,1,0:T(8,128)S(1)}, f32[4,56,128]{2,1,0:T(8,128)S(1)}, u32[]{:S(2)}, u32[]{:S(2)}) collective-permute-start(f32[4,56,128]{2,1,0:T(8,128)S(1)} %get-tuple-element.24), channel_id=1, source_target_pairs={{0,3},{1,2},{2,1},{3,0},{4,7},{5,6},{6,5},{7,4},{8,11},{9,10},{10,... | collective-permute-start | bytes 344072 | tf_op jit(solution)/shard_map/ppermute | solution.py:482
  25.8 5.2 %collective-permute-start.6 = (f32[1,56,128]{2,1,0:T(8,128)S(1)}, f32[1,56,128]{2,1,0:T(8,128)S(1)}, u32[]{:S(2)}, u32[]{:S(2)}) collective-permute-start(f32[1,56,128]{2,1,0:T(8,128)S(1)} %get-tuple-element.27), channel_id=1, source_target_pairs={{0,13},{1,12},{2,15},{3,14},{4,9},{5,8},{6,11},{7,10},{8,5},{9,4},... | collective-permute-start | bytes 86024 | tf_op jit(solution)/shard_map/ppermute | solution.py:490
  29.3 4.8 %collective-permute-start.7 = (f32[1,56,128]{2,1,0:T(8,128)S(1)}, f32[1,56,128]{2,1,0:T(8,128)S(1)}, u32[]{:S(2)}, u32[]{:S(2)}) collective-permute-start(f32[1,56,128]{2,1,0:T(8,128)S(1)} %get-tuple-element.26), channel_id=1, source_target_pairs={{0,8},{1,9},{2,10},{3,11},{4,12},{5,13},{6,14},{7,15},{8,0},{9,1},... | collective-permute-start | bytes 86024 | tf_op jit(solution)/shard_map/ppermute | solution.py:490
  29.3 4.8 %collective-permute-start.8 = (f32[1,56,128]{2,1,0:T(8,128)S(1)}, f32[1,56,128]{2,1,0:T(8,128)S(1)}, u32[]{:S(2)}, u32[]{:S(2)}) collective-permute-start(f32[1,56,128]{2,1,0:T(8,128)S(1)} %get-tuple-element.25), channel_id=1, source_target_pairs={{0,5},{1,4},{2,7},{3,6},{4,1},{5,0},{6,3},{7,2},{8,13},{9,12},{10,... | collective-permute-start | bytes 86024 | tf_op jit(solution)/shard_map/ppermute | solution.py:490
